TPU v7x, 32 devices: a whole 2x2x4 slice. The times are simulated.
32 devices in a mesh: ea: 4 (over y, x), row: 4 (over z), col: 2 (over core).
Axes of the slice: x: 2, y: 2, z: 4, core: 2. Of those that a mesh axis runs over, the one named last changes fastest.
Arguments:
- weights: float32 [4, 256, 2048], P('ea', 'row', 'col'), parts along dimension 0, may hold values from -6 to 6
- codebook: float32 [4, 16, 2, 256], P('ea', 'col'), parts along dimension 0, may hold values from -4 to 4
- assign: int32 [4, 256, 1024], P('ea', 'row', 'col'), parts along dimension 0, may hold values from 0 to 255
- chol_upper: float32 [4, 2048, 2048], P('ea', 'row', 'col'), parts along dimension 0, may hold values from 0 to 1.4, as said below
- inv_blocks: float32 [4, 16, 128, 128], P('ea', 'col'), parts along dimension 0, may hold values from -1 to 1.5, as said below
Outputs:
- errors: float32 [4, 256, 2048], P('ea', 'row', 'col'), parts along dimension 0
- row_loss: float32 [4, 256], P('ea', 'row'), parts along dimension 0
- codeword_mass: float32 [4, 16, 256], P('ea', 'col'), parts along dimension 0
There are 4 independent parts, one for each index of `ea`. A program takes and returns all parts, laid end to end along the dimension named above; each array names one. Nothing has to cross between parts.
Inputs may be any that keep to these rules, and one draw needn't show every extreme that they name: `chol_upper`: upper triangular with a positive diagonal. inv_blocks[x, b] is the inverse of the diagonal block of chol_upper[x] on rows and columns [b * 128, (b + 1) * 128).
All inputs are finite; a program needn't handle non-finite values.
Results may differ from a plain program's by a relative error of at most 0.0001.
Values sent between devices are 32-bit elements; how exact they have to be, the bound alone decides.
A program may use at most 64 MiB of HBM per device.

v0:
```python
import functools

import jax
import jax.numpy as jnp
from jax import lax
from jax.experimental import pallas as pl
from jax.experimental.pallas import tpu as pltpu
from jax.sharding import PartitionSpec as P

F32 = jnp.float32
BF16 = jnp.bfloat16
LOW = 16
PIECES = 2


def halves(value):
    high = value.astype(BF16)
    return high, (value - high.astype(F32)).astype(BF16)


def dot(a, b):
    return jnp.dot(a, b, preferred_element_type=F32)


def dot3(a, b_high, b_low):
    rows = a.shape[0]
    high, low = halves(a)
    both = dot(jnp.concatenate([high, low], axis=0), b_high)
    return both[:rows] + both[rows:] + dot(high, b_low)


def dot_full(a, b):
    b_high, b_low = halves(b)
    return dot3(a, b_high, b_low)


def take(table, index):
    return jnp.take_along_axis(table, index, axis=1, mode="promise_in_bounds")


def kernel(
    nr, nc,
    weights_hbm, codebook_hbm, assign_hbm, inverse_hbm, factor,
    errors_out, loss_out, mass_out,
    weights, codebook, assign, inverse, u_raw, u_high, u_low, v_full, v_high, v_low, delta, codes, delta_in, run_in, run_out,
    err_block, err_own, mass_all, loss_all,
    u_sem, d_send, d_recv, run_send, run_recv, core_send, core_recv, own_send, own_recv,
    mass_send, mass_recv, loss_send, loss_recv,
):
    z = lax.axis_index("row")
    c = lax.axis_index("col")
    rows, width = weights.shape
    span = factor.shape[0]
    m = width // span
    block = inverse.shape[1]
    k = span // block
    code_count = codebook.shape[2]
    owner = z // m
    slot = z % m
    steps = nr * PIECES
    piece = rows // PIECES
    is_owner = c == owner

    def remote(src, dst, send, recv, row, col):
        return pltpu.make_async_remote_copy(
            src_ref=src, dst_ref=dst, send_sem=send, recv_sem=recv,
            device_id={"row": row, "col": col}, device_id_type=pl.DeviceIdType.MESH,
        )

    loads = [
        pltpu.make_async_copy(source, target, u_sem.at[number])
        for number, (source, target) in enumerate((
            (assign_hbm, assign), (codebook_hbm, codebook), (weights_hbm, weights),
            (inverse_hbm, inverse), (factor, u_raw),
        ))
    ]
    for load in loads:
        load.start()

    barrier = pltpu.get_barrier_semaphore()
    for step in range(1, nr * nc):
        other = lax.rem(z * nc + c + step, nr * nc)
        pl.semaphore_signal(
            barrier, inc=1, device_id={"row": other // nc, "col": other % nc},
            device_id_type=pl.DeviceIdType.MESH,
        )

    for load in loads[:3]:
        load.wait()

    lane = lax.broadcasted_iota(jnp.int32, (rows, block), 1)
    for b in range(width // block):
        first = b * (block // 2)
        tile = first // block * block
        code = take(assign[:, tile:tile + block], first - tile + lane // 2)
        codes[b] = code
        inner = code % block
        value = jnp.zeros((rows, block), F32)
        for part in range(code_count // block):
            picked = []
            for comp in range(2):
                table = codebook[b, comp:comp + 1, part * block:(part + 1) * block]
                picked.append(take(jnp.broadcast_to(table, (rows, block)), inner))
            both = jnp.where(lane % 2 == 0, picked[0], picked[1])
            value = jnp.where(code // block == part, both, value)
        j, at = b * block // span, b * block % span
        delta[j, :, at:at + block] = weights[:, b * block:(b + 1) * block] - value

    @pl.when(z == 0)
    def _():
        run_in[...] = jnp.zeros_like(run_in)

    pl.semaphore_wait(barrier, nr * nc - 1)

    def delta_copy(j):
        return remote(delta.at[j], delta_in.at[z], d_send.at[j], d_recv.at[z], c * m + j, c)

    for j in range(m):
        @pl.when(c * m + j < z)
        def _():
            delta_copy(j).start()

    for load in loads[3:]:
        load.wait()

    @pl.when(is_owner)
    def _():
        v_full[...] = jnp.zeros_like(v_full)
        base = slot * span

        def invert(lo, hi):
            if hi - lo == 1:
                v_full[lo * block:hi * block, lo * block:hi * block] = inverse[slot * k + lo]
                return
            mid = (lo + hi) // 2
            invert(lo, mid)
            invert(mid, hi)
            top, middle, end = lo * block, mid * block, hi * block
            right = u_raw[top:middle, pl.ds(pl.multiple_of(base + middle, block), end - middle)]
            product = dot_full(v_full[top:middle, top:middle], right)
            v_full[top:middle, middle:end] = -dot_full(product, v_full[middle:end, middle:end])

        invert(0, k)
        high, low = halves(v_full[...])
        v_high[...] = high
        v_low[...] = low

    for j in range(m):
        @pl.when(c * m + j > z)
        def _():
            high, low = halves(u_raw[:, j * span:(j + 1) * span])
            u_high[:, j * span:(j + 1) * span] = high
            u_low[:, j * span:(j + 1) * span] = low

    def run_copy(g, j):
        return remote(run_out.at[g, j], run_in.at[g, j], run_send.at[g, j], run_recv.at[g, j], z + 1, c)

    def core_copy(g, col):
        return remote(err_block.at[g], err_block.at[g], core_send.at[g, col], core_recv.at[g], z, col)

    def part_rows(q):
        return pl.ds(pl.multiple_of(q % PIECES * piece, piece), piece)

    def own_copy(q):
        return remote(
            err_block.at[q], err_own.at[slot, part_rows(q)],
            own_send.at[q], own_recv.at[slot, q % PIECES], q // PIECES, c,
        )

    def arrived(ref, sem):
        pltpu.make_async_copy(ref, ref, sem).wait()

    def stage(q, _):
        g = q // PIECES
        at = part_rows(q)

        @pl.when(is_owner)
        def _():
            @pl.when(z > 0)
            def _():
                arrived(run_in.at[q, slot], run_recv.at[q, slot])

            @pl.when(g > z)
            def _():
                @pl.when(q % PIECES == 0)
                def _():
                    arrived(delta_in.at[g], d_recv.at[g])

                run_in[q, slot] = run_in[q, slot] + delta_in[g, at]

            @pl.when(g == z)
            def _():
                run_in[q, slot] = run_in[q, slot] + delta[slot, at]

            error = dot3(run_in[q, slot], v_high[...], v_low[...])
            err_block[q] = error

            @pl.when(g == z)
            def _():
                err_own[slot, at] = error

            for col in range(1, nc):
                @pl.when(col > c)
                def _():
                    core_copy(q, col).start()

            @pl.when(g < z)
            def _():
                own_copy(q).start()

        @pl.when(c > owner)
        def _():
            arrived(err_block.at[q], core_recv.at[q])

        for j in range(m):
            @pl.when(c * m + j > z)
            def _():
                change = dot3(
                    err_block[q], u_high[:, j * span:(j + 1) * span], u_low[:, j * span:(j + 1) * span]
                )

                @pl.when(z > 0)
                def _():
                    arrived(run_in.at[q, j], run_recv.at[q, j])

                local = jnp.where(g == z, delta[j, at], 0.0)
                run_out[q, j] = run_in[q, j] + local - change
                run_copy(q, j).start()

        return 0

    lax.fori_loop(0, steps, stage, 0)

    for q in range(PIECES, steps):
        @pl.when(is_owner & (q // PIECES > z))
        def _():
            own_copy(q).start()

    high_count = code_count // LOW
    group = 2 * high_count
    chunk = 8
    loss = jnp.zeros((8, rows), F32)
    for j in range(m):
        @pl.when(c * m + j != z)
        def _():
            for h in range(PIECES):
                arrived(err_own.at[j, h * piece:(h + 1) * piece], own_recv.at[j, h])

        error = err_own[j]
        errors_out[:, j * span:(j + 1) * span] = error
        squared = error * error
        loss = loss + lax.dot_general(
            jnp.ones((8, span), F32), squared, (((1,), (1,)), ((), ())),
            precision=lax.Precision.HIGHEST, preferred_element_type=F32,
        )

        def gather(step, total):
            at = pl.ds(pl.multiple_of(step * chunk, chunk), chunk)
            iota_high = lax.broadcasted_iota(jnp.int32, (high_count, block), 0)
            iota_low = lax.broadcasted_iota(jnp.int32, (LOW, block), 0)
            left, right = [], []
            for b in range(k):
                code = codes[j * k + b, at, :]
                value = err_own[j, at, b * block:(b + 1) * block]
                value = value * value
                coarse = value.astype(BF16).astype(F32)
                fine = value - coarse
                code_high, code_low = code // LOW, code % LOW
                top, bottom, marks = [], [], []
                for r in range(chunk):
                    hit = jnp.broadcast_to(code_high[r:r + 1], (high_count, block)) == iota_high
                    top.append(jnp.where(hit, jnp.broadcast_to(coarse[r:r + 1], (high_count, block)), 0.0).astype(BF16))
                    bottom.append(jnp.where(hit, jnp.broadcast_to(fine[r:r + 1], (high_count, block)), 0.0).astype(BF16))
                    low_hit = jnp.broadcast_to(code_low[r:r + 1], (LOW, block)) == iota_low
                    marks.append(jnp.where(low_hit, 1.0, 0.0).astype(BF16))
                left += [jnp.concatenate(top, axis=1), jnp.concatenate(bottom, axis=1)]
                right.append(jnp.concatenate(marks, axis=1))
            return total + lax.dot_general(
                jnp.concatenate(left, axis=0), jnp.concatenate(right, axis=0),
                (((1,), (1,)), ((), ())), preferred_element_type=F32,
            )

        total = lax.fori_loop(0, rows // chunk, gather, jnp.zeros((k * group, k * LOW), F32), unroll=4)
        row_id = lax.broadcasted_iota(jnp.int32, total.shape, 0)
        col_id = lax.broadcasted_iota(jnp.int32, total.shape, 1)
        total = jnp.where(row_id // group == col_id // LOW, total, 0.0)
        wide_row = lax.broadcasted_iota(jnp.int32, (k * LOW, code_count), 0)
        wide_col = lax.broadcasted_iota(jnp.int32, (k * LOW, code_count), 1)
        spread = jnp.where(wide_row % LOW == wide_col % LOW, 1.0, 0.0)
        spread = jnp.dot(total, spread, precision=lax.Precision.HIGHEST, preferred_element_type=F32)
        out_row = lax.broadcasted_iota(jnp.int32, spread.shape, 0)
        out_col = lax.broadcasted_iota(jnp.int32, spread.shape, 1)
        spread = jnp.where(out_row % high_count == out_col // LOW, spread, 0.0)
        for b in range(k):
            mass_all[z, j * k + b:j * k + b + 1, :] = jnp.sum(
                spread[b * group:(b + 1) * group], axis=0, keepdims=True
            )

    loss_all[c, :, :rows] = loss

    def mass_copy(row):
        return remote(mass_all.at[z], mass_all.at[z], mass_send.at[row], mass_recv.at[z], row, c)

    def loss_copy(col):
        return remote(loss_all.at[c], loss_all.at[c], loss_send.at[col], loss_recv.at[c], z, col)

    for row in range(nr):
        @pl.when(row != z)
        def _():
            mass_copy(row).start()
    for col in range(nc):
        @pl.when(col != c)
        def _():
            loss_copy(col).start()

    for j in range(m):
        @pl.when(c * m + j < z)
        def _():
            delta_copy(j).wait_send()

    def drain(q, _):
        for j in range(m):
            @pl.when(c * m + j > z)
            def _():
                run_copy(q, j).wait_send()

        @pl.when(is_owner)
        def _():
            for col in range(1, nc):
                @pl.when(col > c)
                def _():
                    core_copy(q, col).wait_send()

            @pl.when(q // PIECES != z)
            def _():
                own_copy(q).wait_send()

        return 0

    lax.fori_loop(0, steps, drain, 0)

    for col in range(nc):
        @pl.when(col != c)
        def _():
            arrived(loss_all.at[col], loss_recv.at[col])
    loss_sum = loss_all[0, 0:1, :rows]
    for col in range(1, nc):
        loss_sum = loss_sum + loss_all[col, 0:1, :rows]
    loss_out[...] = loss_sum
    for row in range(nr):
        @pl.when(row != z)
        def _():
            arrived(mass_all.at[row], mass_recv.at[row])
    mass_sum = mass_all[0]
    for row in range(1, nr):
        mass_sum = mass_sum + mass_all[row]
    mass_out[...] = mass_sum

    for row in range(nr):
        @pl.when(row != z)
        def _():
            mass_copy(row).wait_send()
    for col in range(nc):
        @pl.when(col != c)
        def _():
            loss_copy(col).wait_send()


def local(nr, nc, weights, codebook, assign, chol_upper, inv_blocks):
    rows, width = weights.shape[1:]
    span = chol_upper.shape[1]
    m = width // span
    steps, piece = nr * PIECES, rows // PIECES
    blocks, code_count = codebook.shape[1], codebook.shape[3]
    block = inv_blocks.shape[2]
    dma = pltpu.SemaphoreType.DMA
    vmem = pl.BlockSpec(memory_space=pltpu.VMEM)
    errors, loss, mass = pl.pallas_call(
        functools.partial(kernel, nr, nc),
        out_shape=(
            jax.ShapeDtypeStruct((rows, width), F32),
            jax.ShapeDtypeStruct((1, rows), F32),
            jax.ShapeDtypeStruct((blocks, code_count), F32),
        ),
        in_specs=[pl.BlockSpec(memory_space=pl.ANY)] * 5,
        out_specs=(vmem, vmem, vmem),
        scratch_shapes=[
            pltpu.VMEM(weights.shape[1:], F32),
            pltpu.VMEM(codebook.shape[1:], F32),
            pltpu.VMEM(assign.shape[1:], jnp.int32),
            pltpu.VMEM(inv_blocks.shape[1:], F32),
            pltpu.VMEM((span, width), F32),
            pltpu.VMEM((span, width), BF16),
            pltpu.VMEM((span, width), BF16),
            pltpu.VMEM((span, span), F32),
            pltpu.VMEM((span, span), BF16),
            pltpu.VMEM((span, span), BF16),
            pltpu.VMEM((m, rows, span), F32),
            pltpu.VMEM((blocks, rows, block), jnp.int32),
            pltpu.VMEM((nr, rows, span), F32),
            pltpu.VMEM((steps, m, piece, span), F32),
            pltpu.VMEM((steps, m, piece, span), F32),
            pltpu.VMEM((steps, piece, span), F32),
            pltpu.VMEM((m, rows, span), F32),
            pltpu.VMEM((nr, blocks, code_count), F32),
            pltpu.VMEM((nc, 8, max(rows, 128)), F32),
            dma((5,)),
            dma((m,)), dma((nr,)),
            dma((steps, m)), dma((steps, m)),
            dma((steps, nc)), dma((steps,)),
            dma((steps,)), dma((m, PIECES)),
            dma((nr,)), dma((nr,)),
            dma((nc,)), dma((nc,)),
        ],
        compiler_params=pltpu.CompilerParams(
            collective_id=0, has_side_effects=True, vmem_limit_bytes=62 * 1024 * 1024
        ),
    )(weights[0], codebook[0], assign[0], inv_blocks[0], chol_upper[0])
    return errors[None], loss, mass[None]


def solution(mesh):
    return jax.shard_map(
        functools.partial(local, mesh.shape["row"], mesh.shape["col"]),
        mesh=mesh,
        in_specs=(
            P("ea", "row", "col"),
            P("ea", "col", None, None),
            P("ea", "row", "col"),
            P("ea", "row", "col"),
            P("ea", "col", None, None),
        ),
        out_specs=(P("ea", "row", "col"), P("ea", "row"), P("ea", "col", None)),
        check_vma=False,
    )
```

profile of v0, /device:TPU:1, one launch (start us, length us, event | category | flops | bytes accessed | tf_op | source)
XLA Modules:
  0.0 51.4 jit_solution(12532777958247598898)
XLA Ops:
  0.6 46.7 %shard_map.76 = (f32[64,1024]{1,0:T(8,128)}, f32[1,64]{1,0:T(1,128)}, f32[8,256]{1,0:T(8,128)}) custom-call(f32[64,1024]{1,0:T(8,128)} %bitcast.9, f32[8,2,256]{2,1,0:T(2,128)} %bitcast.12, s32[64,512]{1,0:T(8,128)} %bitcast.11, f32[8,128,128]{2,1,0:T(8,128)} %bitcast.8, f32[512,1024]{1,0:T(8,128)} %bitcast.7), custom_call_target="tpu_custom_call" | custom-call | tf_op jit(solution)/shard_map/pallas_call | solution.py:378
  47.4 1.7 %copy.11 = f32[1,64,1024]{2,1,0:T(8,128)} copy(f32[1,64,1024]{2,1,0:T(8,128)} %bitcast.10) | data formatting | bytes 524288
  49.0 1.1 %copy.12 = f32[1,64]{1,0:T(1,128)} copy(f32[1,64]{1,0:T(1,128)} %get-tuple-element.13) | data formatting | bytes 512
  50.1 1.3 %copy.13 = f32[1,8,256]{2,1,0:T(8,128)} copy(f32[1,8,256]{2,1,0:T(8,128)} %bitcast.13) | data formatting | bytes 16384
where the time goes:
time: 51.6 us; the launch traced here: 51.4 us
  Pallas kernels  46.7 us (91%)
  local copies, waits for them, and re-layouts  4.05 us (8%)
  between operations  0.64 us (1%)
    pallas_call x1, Pallas kernels, local(): pl.pallas_call(functools.partial(kernel, nr, nc), out_shape=(jax.ShapeDty...  46.7 us
    unnamed x3, local copies, waits for them, and re-layouts  4.05 us

commit v1 on v0

--- a/solution.py
+++ b/solution.py
@@ -11,6 +11,7 @@
 BF16 = jnp.bfloat16
 LOW = 16
 PIECES = 2
+scope = jax.named_scope
 
 
 def halves(value):
@@ -85,8 +86,9 @@
             device_id_type=pl.DeviceIdType.MESH,
         )
 
-    for load in loads[:3]:
-        load.wait()
+    with scope("first_loads"):
+        for load in loads[:3]:
+            load.wait()
 
     lane = lax.broadcasted_iota(jnp.int32, (rows, block), 1)
     for b in range(width // block):
@@ -110,7 +112,10 @@
     def _():
         run_in[...] = jnp.zeros_like(run_in)
 
-    pl.semaphore_wait(barrier, nr * nc - 1)
+    @pl.when(z > 0)
+    def _():
+        with scope("entry"):
+            pl.semaphore_wait(barrier, nr * nc - 1)
 
     def delta_copy(j):
         return remote(delta.at[j], delta_in.at[z], d_send.at[j], d_recv.at[z], c * m + j, c)
@@ -120,8 +125,9 @@
         def _():
             delta_copy(j).start()
 
-    for load in loads[3:]:
-        load.wait()
+    with scope("factor_loads"):
+        for load in loads[3:]:
+            load.wait()
 
     @pl.when(is_owner)
     def _():
@@ -152,6 +158,11 @@
             u_high[:, j * span:(j + 1) * span] = high
             u_low[:, j * span:(j + 1) * span] = low
 
+    @pl.when(z == 0)
+    def _():
+        with scope("entry"):
+            pl.semaphore_wait(barrier, nr * nc - 1)
+
     def run_copy(g, j):
         return remote(run_out.at[g, j], run_in.at[g, j], run_send.at[g, j], run_recv.at[g, j], z + 1, c)
 
@@ -164,11 +175,14 @@
     def own_copy(q):
         return remote(
             err_block.at[q], err_own.at[slot, part_rows(q)],
-            own_send.at[q], own_recv.at[slot, q % PIECES], q // PIECES, c,
+            own_send.at[q], own_recv.at[slot, q % PIECES], q // PIECES, owner,
         )
 
     def arrived(ref, sem):
         pltpu.make_async_copy(ref, ref, sem).wait()
+
+    def held(q, j):
+        return (c > owner) & (q >= PIECES) & (j > 0)
 
     def stage(q, _):
         g = q // PIECES
@@ -178,13 +192,15 @@
         def _():
             @pl.when(z > 0)
             def _():
-                arrived(run_in.at[q, slot], run_recv.at[q, slot])
+                with scope("wait_own_sum"):
+                    arrived(run_in.at[q, slot], run_recv.at[q, slot])
 
             @pl.when(g > z)
             def _():
                 @pl.when(q % PIECES == 0)
                 def _():
-                    arrived(delta_in.at[g], d_recv.at[g])
+                    with scope("wait_delta"):
+                        arrived(delta_in.at[g], d_recv.at[g])
 
                 run_in[q, slot] = run_in[q, slot] + delta_in[g, at]
 
@@ -210,7 +226,8 @@
 
         @pl.when(c > owner)
         def _():
-            arrived(err_block.at[q], core_recv.at[q])
+            with scope("wait_core"):
+                arrived(err_block.at[q], core_recv.at[q])
 
         for j in range(m):
             @pl.when(c * m + j > z)
@@ -218,36 +235,71 @@
                 change = dot3(
                     err_block[q], u_high[:, j * span:(j + 1) * span], u_low[:, j * span:(j + 1) * span]
                 )
-
+                local = jnp.where(g == z, delta[j, at], 0.0)
+                later = held(q, j)
+
+                @pl.when(later)
+                def _():
+                    run_out[q, j] = local - change
+
+                @pl.when(jnp.logical_not(later))
+                def _():
+                    @pl.when(z > 0)
+                    def _():
+                        with scope("wait_near_sum"):
+                            arrived(run_in.at[q, j], run_recv.at[q, j])
+
+                    run_out[q, j] = run_in[q, j] + local - change
+                    run_copy(q, j).start()
+
+        return 0
+
+    lax.fori_loop(0, steps, stage, 0)
+
+    for j in range(1, m):
+        @pl.when((c * m + j > z) & (c > owner))
+        def _():
+            def release(q, _):
                 @pl.when(z > 0)
                 def _():
-                    arrived(run_in.at[q, j], run_recv.at[q, j])
-
-                local = jnp.where(g == z, delta[j, at], 0.0)
-                run_out[q, j] = run_in[q, j] + local - change
+                    with scope("wait_far_sum"):
+                        arrived(run_in.at[q, j], run_recv.at[q, j])
+                    run_out[q, j] = run_out[q, j] + run_in[q, j]
+
                 run_copy(q, j).start()
-
-        return 0
-
-    lax.fori_loop(0, steps, stage, 0)
-
-    for q in range(PIECES, steps):
-        @pl.when(is_owner & (q // PIECES > z))
-        def _():
-            own_copy(q).start()
+                return 0
+
+            lax.fori_loop(PIECES, steps, release, 0)
+
+    @pl.when(c == nc - 1)
+    def _():
+        def upward(i, _):
+            q = steps - 1 - i
+
+            @pl.when(q // PIECES > z)
+            def _():
+                own_copy(q).start()
+
+            return 0
+
+        lax.fori_loop(0, steps, upward, 0)
 
     high_count = code_count // LOW
     group = 2 * high_count
     chunk = 8
-    loss = jnp.zeros((8, rows), F32)
-    for j in range(m):
+    start = jnp.clip(z - c * m, 0, m - 1)
+
+    def finish(turn, loss):
+        j = lax.rem(start + turn, m)
+
         @pl.when(c * m + j != z)
         def _():
-            for h in range(PIECES):
-                arrived(err_own.at[j, h * piece:(h + 1) * piece], own_recv.at[j, h])
+            with scope("wait_error"):
+                for h in range(PIECES):
+                    arrived(err_own.at[j, h * piece:(h + 1) * piece], own_recv.at[j, h])
 
         error = err_own[j]
-        errors_out[:, j * span:(j + 1) * span] = error
+        errors_out[:, pl.ds(pl.multiple_of(j * span, span), span)] = error
         squared = error * error
         loss = loss + lax.dot_general(
             jnp.ones((8, span), F32), squared, (((1,), (1,)), ((), ())),
@@ -292,11 +344,12 @@
         out_col = lax.broadcasted_iota(jnp.int32, spread.shape, 1)
         spread = jnp.where(out_row % high_count == out_col // LOW, spread, 0.0)
         for b in range(k):
-            mass_all[z, j * k + b:j * k + b + 1, :] = jnp.sum(
+            mass_all[z, pl.ds(j * k + b, 1), :] = jnp.sum(
                 spread[b * group:(b + 1) * group], axis=0, keepdims=True
             )
-
-    loss_all[c, :, :rows] = loss
+        return loss
+
+    loss_all[c, :, :rows] = lax.fori_loop(0, m, finish, jnp.zeros((8, rows), F32))
 
     def mass_copy(row):
         return remote(mass_all.at[z], mass_all.at[z], mass_send.at[row], mass_recv.at[z], row, c)
@@ -331,18 +384,20 @@
                 def _():
                     core_copy(q, col).wait_send()
 
-            @pl.when(q // PIECES != z)
-            def _():
-                own_copy(q).wait_send()
+        @pl.when((is_owner & (q // PIECES < z)) | ((c == nc - 1) & (q // PIECES > z)))
+        def _():
+            own_copy(q).wait_send()
 
         return 0
 
-    lax.fori_loop(0, steps, drain, 0)
+    with scope("drain"):
+        lax.fori_loop(0, steps, drain, 0)
 
     for col in range(nc):
         @pl.when(col != c)
         def _():
-            arrived(loss_all.at[col], loss_recv.at[col])
+            with scope("wait_loss"):
+                arrived(loss_all.at[col], loss_recv.at[col])
     loss_sum = loss_all[0, 0:1, :rows]
     for col in range(1, nc):
         loss_sum = loss_sum + loss_all[col, 0:1, :rows]
@@ -350,7 +405,8 @@
     for row in range(nr):
         @pl.when(row != z)
         def _():
-            arrived(mass_all.at[row], mass_recv.at[row])
+            with scope("wait_mass"):
+                arrived(mass_all.at[row], mass_recv.at[row])
     mass_sum = mass_all[0]
     for row in range(1, nr):
         mass_sum = mass_sum + mass_all[row]
@@ -364,6 +420,17 @@
         @pl.when(col != c)
         def _():
             loss_copy(col).wait_send()
+
+
+def store(errors, loss, mass, errors_out, loss_out, mass_out, sems):
+    copies = [
+        pltpu.make_async_copy(source, target, sems.at[number])
+        for number, (source, target) in enumerate(((errors, errors_out), (loss, loss_out), (mass, mass_out)))
+    ]
+    for copy in copies:
+        copy.start()
+    for copy in copies:
+        copy.wait()
 
 
 def local(nr, nc, weights, codebook, assign, chol_upper, inv_blocks):
@@ -375,14 +442,11 @@
     block = inv_blocks.shape[2]
     dma = pltpu.SemaphoreType.DMA
     vmem = pl.BlockSpec(memory_space=pltpu.VMEM)
-    errors, loss, mass = pl.pallas_call(
+    shapes = ((rows, width), (1, rows), (blocks, code_count))
+    results = pl.pallas_call(
         functools.partial(kernel, nr, nc),
-        out_shape=(
-            jax.ShapeDtypeStruct((rows, width), F32),
-            jax.ShapeDtypeStruct((1, rows), F32),
-            jax.ShapeDtypeStruct((blocks, code_count), F32),
-        ),
-        in_specs=[pl.BlockSpec(memory_space=pl.ANY)] * 5,
+        out_shape=tuple(pltpu.VMEM(shape, F32) for shape in shapes),
+        in_specs=[pl.BlockSpec(memory_space=pltpu.HBM)] * 5,
         out_specs=(vmem, vmem, vmem),
         scratch_shapes=[
             pltpu.VMEM(weights.shape[1:], F32),
@@ -413,9 +477,19 @@
             dma((nc,)), dma((nc,)),
         ],
         compiler_params=pltpu.CompilerParams(
-            collective_id=0, has_side_effects=True, vmem_limit_bytes=62 * 1024 * 1024
+            collective_id=0, has_side_effects=True, vmem_limit_bytes=40 * 1024 * 1024
         ),
-    )(weights[0], codebook[0], assign[0], inv_blocks[0], chol_upper[0])
+    )(*(pltpu.with_memory_space_constraint(value[0], pltpu.HBM) for value in (
+        weights, codebook, assign, inv_blocks, chol_upper,
+    )))
+    errors, loss, mass = pl.pallas_call(
+        store,
+        out_shape=tuple(jax.ShapeDtypeStruct(shape, F32) for shape in shapes),
+        in_specs=[vmem] * 3,
+        out_specs=[pl.BlockSpec(memory_space=pltpu.HBM)] * 3,
+        scratch_shapes=[dma((3,))],
+        compiler_params=pltpu.CompilerParams(vmem_limit_bytes=1024 * 1024),
+    )(*results)
     return errors[None], loss, mass[None]
 
 

time: 51.6 us -> 45.7 us (0.89)
  local copies, waits for them, and re-layouts: 4.05 us -> 0 us
  Pallas kernels: 46.7 us -> 44.9 us
    unnamed x3 -> x0, local copies, waits for them, and re-layouts: 4.05 us -> none
    pallas_call x1 -> x2, Pallas kernels: 46.7 us -> 44.9 us  [the longest x1 44.2 us: local(): pl.pallas_call(functools.partial(kernel, nr, nc), out_shape=tuple((pltpu....]
where the time goes in v1:
time: 45.7 us; the launch traced here: 45.5 us
  Pallas kernels  44.9 us (98%)
  between operations  0.64 us (1%)
    pallas_call x1, Pallas kernels, local(): pl.pallas_call(functools.partial(kernel, nr, nc), out_shape=tuple((pltpu....  44.2 us

profile of v1, /device:TPU:1, one launch (start us, length us, event | category | flops | bytes accessed | tf_op | source)
XLA Modules:
  0.0 45.5 jit_solution(7695485796085165551)
XLA Ops:
  0.6 44.2 %shard_map.76 = (f32[64,1024]{1,0:T(8,128)S(1)}, f32[1,64]{1,0:T(1,128)S(1)}, f32[8,256]{1,0:T(8,128)S(1)}) custom-call(f32[64,1024]{1,0:T(8,128)} %bitcast.9, f32[8,2,256]{2,1,0:T(2,128)} %bitcast.11, s32[64,512]{1,0:T(8,128)} %bitcast.10, f32[8,128,128]{2,1,0:T(8,128)} %bitcast.8, f32[512,1024]{1,0:T(8,128)} %bitcast.7), custom_call_target="tpu_custom_call" | custom-call | tf_op jit(solution)/shard_map/pallas_call | solution.py:446
  44.8 0.7 %shard_map.77 = (f32[64,1024]{1,0:T(8,128)}, f32[1,64]{1,0:T(1,128)}, f32[8,256]{1,0:T(8,128)}) custom-call(f32[64,1024]{1,0:T(8,128)S(1)} %get-tuple-element.9.errors, f32[1,64]{1,0:T(1,128)S(1)} %get-tuple-element.10.loss, f32[8,256]{1,0:T(8,128)S(1)} %get-tuple-element.11.mass), custom_call_target="tpu_custom_call" | custom-call | tf_op jit(solution)/shard_map/pallas_call | solution.py:485

commit v2 on v1

--- a/solution.py
+++ b/solution.py
@@ -43,10 +43,11 @@
     nr, nc,
     weights_hbm, codebook_hbm, assign_hbm, inverse_hbm, factor,
     errors_out, loss_out, mass_out,
-    weights, codebook, assign, inverse, u_raw, u_high, u_low, v_full, v_high, v_low, delta, codes, delta_in, run_in, run_out,
-    err_block, err_own, mass_all, loss_all,
-    u_sem, d_send, d_recv, run_send, run_recv, core_send, core_recv, own_send, own_recv,
-    mass_send, mass_recv, loss_send, loss_recv,
+    weights, codebook, assign, inverse, u_raw, u_high, u_low, triangle, v_full, v_high, v_low, w_high, w_low,
+    delta, codes, delta_in, codes_in, run_in, run_out, last_in, last_out,
+    err_block, err_own, tally, mass_all, mass_own, mass_sent, loss_all,
+    u_sem, d_send, d_recv, code_send, code_recv, tri_send, tri_recv, run_send, run_recv, last_send, last_recv,
+    core_send, core_recv, own_send, own_recv, part_send, part_recv, mass_send, mass_recv, loss_send, loss_recv,
 ):
     z = lax.axis_index("row")
     c = lax.axis_index("col")
@@ -60,13 +61,18 @@
     slot = z % m
     steps = nr * PIECES
     piece = rows // PIECES
-    is_owner = c == owner
+    final = nr - 1
+    is_owner = (c == owner) & (z < final)
+    is_last = c == nc - 1
 
     def remote(src, dst, send, recv, row, col):
         return pltpu.make_async_remote_copy(
             src_ref=src, dst_ref=dst, send_sem=send, recv_sem=recv,
             device_id={"row": row, "col": col}, device_id_type=pl.DeviceIdType.MESH,
         )
+
+    def arrived(ref, sem):
+        pltpu.make_async_copy(ref, ref, sem).wait()
 
     loads = [
         pltpu.make_async_copy(source, target, u_sem.at[number])
@@ -84,6 +90,55 @@
         pl.semaphore_signal(
             barrier, inc=1, device_id={"row": other // nc, "col": other % nc},
             device_id_type=pl.DeviceIdType.MESH,
+        )
+
+    def enter():
+        with scope("entry"):
+            pl.semaphore_wait(barrier, nr * nc - 1)
+
+    def order(place):
+        if nr < 3:
+            return place
+        return jnp.where(place == nr - 2, nr - 1, jnp.where(place == nr - 1, nr - 2, place))
+
+    def group(q):
+        return order(q // PIECES)
+
+    def part_rows(q):
+        return pl.ds(pl.multiple_of(q % PIECES * piece, piece), piece)
+
+    def delta_copy(j):
+        return remote(delta.at[j], delta_in.at[z], d_send.at[j], d_recv.at[z], c * m + j, c)
+
+    def code_copy(j):
+        return remote(codes.at[j * k:(j + 1) * k], codes_in.at[z], code_send.at[j], code_recv.at[z], c * m + j, 0)
+
+    def code_sent(j):
+        return (c * m + j <= z) & (c * m + j < final) & ((c > 0) | (c * m + j < z))
+
+    def tri_copy(row, i):
+        low = (m - 1) * span
+        return remote(
+            u_raw.at[i * block:(i + 1) * block, low + (i + 1) * block:low + span],
+            triangle.at[i * block:(i + 1) * block, (i + 1) * block:span],
+            tri_send.at[row, i], tri_recv.at[i], row, c,
+        )
+
+    def run_copy(q, j):
+        return remote(run_out.at[q, j], run_in.at[q, j], run_send.at[q, j], run_recv.at[q, j], z + 1, c)
+
+    def last_copy(q):
+        return remote(
+            last_out.at[q], last_in.at[z, q % PIECES], last_send.at[q], last_recv.at[z, q % PIECES], group(q), c
+        )
+
+    def core_copy(q, col):
+        return remote(err_block.at[q], err_block.at[q], core_send.at[q, col], core_recv.at[q], z, col)
+
+    def own_copy(q):
+        return remote(
+            err_block.at[q], err_own.at[slot, part_rows(q)],
+            own_send.at[q], own_recv.at[slot, q % PIECES], group(q), owner,
         )
 
     with scope("first_loads"):
@@ -108,17 +163,9 @@
         j, at = b * block // span, b * block % span
         delta[j, :, at:at + block] = weights[:, b * block:(b + 1) * block] - value
 
-    @pl.when(z == 0)
-    def _():
-        run_in[...] = jnp.zeros_like(run_in)
-
     @pl.when(z > 0)
     def _():
-        with scope("entry"):
-            pl.semaphore_wait(barrier, nr * nc - 1)
-
-    def delta_copy(j):
-        return remote(delta.at[j], delta_in.at[z], d_send.at[j], d_recv.at[z], c * m + j, c)
+        enter()
 
     for j in range(m):
         @pl.when(c * m + j < z)
@@ -129,25 +176,35 @@
         for load in loads[3:]:
             load.wait()
 
-    @pl.when(is_owner)
-    def _():
+    @pl.when((z == final) & is_last)
+    def _():
+        for row in reversed(range(final)):
+            for i in range(k - 1):
+                tri_copy(row, i).start()
+
+    def inverted(first, right):
         v_full[...] = jnp.zeros_like(v_full)
-        base = slot * span
 
         def invert(lo, hi):
             if hi - lo == 1:
-                v_full[lo * block:hi * block, lo * block:hi * block] = inverse[slot * k + lo]
+                v_full[lo * block:hi * block, lo * block:hi * block] = inverse[first + lo]
                 return
             mid = (lo + hi) // 2
             invert(lo, mid)
             invert(mid, hi)
             top, middle, end = lo * block, mid * block, hi * block
-            right = u_raw[top:middle, pl.ds(pl.multiple_of(base + middle, block), end - middle)]
-            product = dot_full(v_full[top:middle, top:middle], right)
+            product = dot_full(v_full[top:middle, top:middle], right(top, middle, end))
             v_full[top:middle, middle:end] = -dot_full(product, v_full[middle:end, middle:end])
 
         invert(0, k)
-        high, low = halves(v_full[...])
+        return halves(v_full[...])
+
+    @pl.when(is_owner)
+    def _():
+        base = slot * span
+        high, low = inverted(slot * k, lambda top, middle, end: u_raw[
+            top:middle, pl.ds(pl.multiple_of(base + middle, block), end - middle)
+        ])
         v_high[...] = high
         v_low[...] = low
 
@@ -158,38 +215,51 @@
             u_high[:, j * span:(j + 1) * span] = high
             u_low[:, j * span:(j + 1) * span] = low
 
+    def invert_last():
+        @pl.when(z == final)
+        def _():
+            triangle[...] = u_raw[:, (m - 1) * span:]
+
+        @pl.when(z < final)
+        def _():
+            with scope("wait_triangle"):
+                for i in range(k - 1):
+                    part = triangle.at[i * block:(i + 1) * block, (i + 1) * block:span]
+                    arrived(part, tri_recv.at[i])
+
+        high, low = inverted((m - 1) * k, lambda top, middle, end: triangle[top:middle, middle:end])
+        w_high[...] = high
+        w_low[...] = low
+
     @pl.when(z == 0)
     def _():
-        with scope("entry"):
-            pl.semaphore_wait(barrier, nr * nc - 1)
-
-    def run_copy(g, j):
-        return remote(run_out.at[g, j], run_in.at[g, j], run_send.at[g, j], run_recv.at[g, j], z + 1, c)
-
-    def core_copy(g, col):
-        return remote(err_block.at[g], err_block.at[g], core_send.at[g, col], core_recv.at[g], z, col)
-
-    def part_rows(q):
-        return pl.ds(pl.multiple_of(q % PIECES * piece, piece), piece)
-
-    def own_copy(q):
-        return remote(
-            err_block.at[q], err_own.at[slot, part_rows(q)],
-            own_send.at[q], own_recv.at[slot, q % PIECES], q // PIECES, owner,
-        )
-
-    def arrived(ref, sem):
-        pltpu.make_async_copy(ref, ref, sem).wait()
-
-    def held(q, j):
-        return (c > owner) & (q >= PIECES) & (j > 0)
+        enter()
+
+    for j in range(m):
+        @pl.when(code_sent(j))
+        def _():
+            code_copy(j).start()
+
+        @pl.when((c == 0) & (z == j) & (z < final))
+        def _():
+            codes_in[z] = codes[j * k:(j + 1) * k]
+
+    late_core = (z == 0) & (c > owner)
 
     def stage(q, _):
-        g = q // PIECES
+        g = group(q)
         at = part_rows(q)
 
+        @pl.when(is_last & (((z == final) & (q == 0)) | ((z == final - 1) & (q == PIECES))))
+        def _():
+            invert_last()
+
         @pl.when(is_owner)
         def _():
+            @pl.when(z == 0)
+            def _():
+                run_in[q, slot] = jnp.zeros((piece, span), F32)
+
             @pl.when(z > 0)
             def _():
                 with scope("wait_own_sum"):
@@ -215,8 +285,8 @@
             def _():
                 err_own[slot, at] = error
 
-            for col in range(1, nc):
-                @pl.when(col > c)
+            for col in range(nc):
+                @pl.when((col > c) | ((col == 0) & (c > 0) & (g >= z)))
                 def _():
                     core_copy(q, col).start()
 
@@ -224,59 +294,78 @@
             def _():
                 own_copy(q).start()
 
-        @pl.when(c > owner)
+        @pl.when((c > owner) & (z < final))
         def _():
             with scope("wait_core"):
                 arrived(err_block.at[q], core_recv.at[q])
 
+        late = late_core & (q >= PIECES)
         for j in range(m):
-            @pl.when(c * m + j > z)
+            target = c * m + j
+
+            @pl.when((target > z) & (target < final))
             def _():
                 change = dot3(
                     err_block[q], u_high[:, j * span:(j + 1) * span], u_low[:, j * span:(j + 1) * span]
                 )
-                local = jnp.where(g == z, delta[j, at], 0.0)
-                later = held(q, j)
-
-                @pl.when(later)
-                def _():
-                    run_out[q, j] = local - change
-
-                @pl.when(jnp.logical_not(later))
-                def _():
-                    @pl.when(z > 0)
-                    def _():
-                        with scope("wait_near_sum"):
-                            arrived(run_in.at[q, j], run_recv.at[q, j])
-
-                    run_out[q, j] = run_in[q, j] + local - change
-                    run_copy(q, j).start()
-
-        return 0
-
-    lax.fori_loop(0, steps, stage, 0)
-
-    for j in range(1, m):
-        @pl.when((c * m + j > z) & (c > owner))
-        def _():
-            def release(q, _):
+                run_out[q, j] = jnp.where(g == z, delta[j, at], 0.0) - change
+
                 @pl.when(z > 0)
                 def _():
-                    with scope("wait_far_sum"):
+                    with scope("wait_near_sum"):
                         arrived(run_in.at[q, j], run_recv.at[q, j])
                     run_out[q, j] = run_out[q, j] + run_in[q, j]
 
+                @pl.when(jnp.logical_not(late))
+                def _():
+                    run_copy(q, j).start()
+
+        @pl.when(is_last & (z < final))
+        def _():
+            j = m - 1
+            change = dot3(
+                err_block[q], u_high[:, j * span:(j + 1) * span], u_low[:, j * span:(j + 1) * span]
+            )
+
+            @pl.when(g == z)
+            def _():
+                last_in[z, q % PIECES] = change
+
+            @pl.when(g != z)
+            def _():
+                last_out[q] = change
+
+                @pl.when(jnp.logical_not(late))
+                def _():
+                    last_copy(q).start()
+
+        return 0
+
+    lax.fori_loop(0, steps, stage, 0)
+
+    for j in range(m):
+        @pl.when(late_core & (c * m + j < final))
+        def _():
+            def release(q, _):
                 run_copy(q, j).start()
                 return 0
 
             lax.fori_loop(PIECES, steps, release, 0)
 
-    @pl.when(c == nc - 1)
+    @pl.when(late_core & is_last)
+    def _():
+        def release(i, _):
+            last_copy(steps - 1 - i).start()
+            return 0
+
+        lax.fori_loop(0, steps - PIECES, release, 0)
+
+    @pl.when(is_last & (z < final))
     def _():
         def upward(i, _):
             q = steps - 1 - i
 
-            @pl.when(q // PIECES > z)
+            @pl.when(group(q) > z)
             def _():
                 own_copy(q).start()
 
@@ -284,36 +373,23 @@
 
         lax.fori_loop(0, steps, upward, 0)
 
+    @pl.when(is_last & (z < final - 1))
+    def _():
+        invert_last()
+
     high_count = code_count // LOW
-    group = 2 * high_count
+    fold = 2 * high_count
     chunk = 8
-    start = jnp.clip(z - c * m, 0, m - 1)
-
-    def finish(turn, loss):
-        j = lax.rem(start + turn, m)
-
-        @pl.when(c * m + j != z)
-        def _():
-            with scope("wait_error"):
-                for h in range(PIECES):
-                    arrived(err_own.at[j, h * piece:(h + 1) * piece], own_recv.at[j, h])
-
-        error = err_own[j]
-        errors_out[:, pl.ds(pl.multiple_of(j * span, span), span)] = error
-        squared = error * error
-        loss = loss + lax.dot_general(
-            jnp.ones((8, span), F32), squared, (((1,), (1,)), ((), ())),
-            precision=lax.Precision.HIGHEST, preferred_element_type=F32,
-        )
-
+
+    def count(error_at, code_at):
         def gather(step, total):
             at = pl.ds(pl.multiple_of(step * chunk, chunk), chunk)
             iota_high = lax.broadcasted_iota(jnp.int32, (high_count, block), 0)
             iota_low = lax.broadcasted_iota(jnp.int32, (LOW, block), 0)
             left, right = [], []
             for b in range(k):
-                code = codes[j * k + b, at, :]
-                value = err_own[j, at, b * block:(b + 1) * block]
+                code = code_at(b)[at, :]
+                value = error_at[at, b * block:(b + 1) * block]
                 value = value * value
                 coarse = value.astype(BF16).astype(F32)
                 fine = value - coarse
@@ -332,24 +408,105 @@
                 (((1,), (1,)), ((), ())), preferred_element_type=F32,
             )
 
-        total = lax.fori_loop(0, rows // chunk, gather, jnp.zeros((k * group, k * LOW), F32), unroll=4)
+        total = lax.fori_loop(0, piece // chunk, gather, jnp.zeros(tally.shape, F32), unroll=4)
+        tally[...] = tally[...] + total
+
+    def spread(store):
+        total = tally[...]
         row_id = lax.broadcasted_iota(jnp.int32, total.shape, 0)
         col_id = lax.broadcasted_iota(jnp.int32, total.shape, 1)
-        total = jnp.where(row_id // group == col_id // LOW, total, 0.0)
+        total = jnp.where(row_id // fold == col_id // LOW, total, 0.0)
         wide_row = lax.broadcasted_iota(jnp.int32, (k * LOW, code_count), 0)
         wide_col = lax.broadcasted_iota(jnp.int32, (k * LOW, code_count), 1)
-        spread = jnp.where(wide_row % LOW == wide_col % LOW, 1.0, 0.0)
-        spread = jnp.dot(total, spread, precision=lax.Precision.HIGHEST, preferred_element_type=F32)
-        out_row = lax.broadcasted_iota(jnp.int32, spread.shape, 0)
-        out_col = lax.broadcasted_iota(jnp.int32, spread.shape, 1)
-        spread = jnp.where(out_row % high_count == out_col // LOW, spread, 0.0)
+        wide = jnp.where(wide_row % LOW == wide_col % LOW, 1.0, 0.0)
+        wide = jnp.dot(total, wide, precision=lax.Precision.HIGHEST, preferred_element_type=F32)
+        out_row = lax.broadcasted_iota(jnp.int32, wide.shape, 0)
+        out_col = lax.broadcasted_iota(jnp.int32, wide.shape, 1)
+        wide = jnp.where(out_row % high_count == out_col // LOW, wide, 0.0)
         for b in range(k):
-            mass_all[z, pl.ds(j * k + b, 1), :] = jnp.sum(
-                spread[b * group:(b + 1) * group], axis=0, keepdims=True
-            )
-        return loss
-
-    loss_all[c, :, :rows] = lax.fori_loop(0, m, finish, jnp.zeros((8, rows), F32))
+            store(b, jnp.sum(wide[b * fold:(b + 1) * fold], axis=0, keepdims=True))
+        tally[...] = jnp.zeros_like(tally)
+
+    tally[...] = jnp.zeros_like(tally)
+    mass_all[z] = jnp.zeros(mass_all.shape[1:], F32)
+    counts = (c == 0) & (z < final)
+
+    def part_copy(row):
+        return remote(mass_sent, mass_own.at[slot], part_send.at[row], part_recv.at[slot], row, owner)
+
+    def part_remote(row):
+        return counts & ((row != z) | (owner != 0))
+
+    @pl.when(counts)
+    def _():
+        def own_part(q, _):
+            g = group(q)
+
+            @pl.when(g >= z)
+            def _():
+                with scope("wait_part"):
+                    @pl.when(owner != 0)
+                    def _():
+                        arrived(err_block.at[q], core_recv.at[q])
+
+                    @pl.when(((g != z) | (owner != 0)) & (q % PIECES == 0))
+                    def _():
+                        arrived(codes_in.at[g], code_recv.at[g])
+
+                count(err_block.at[q], lambda b: codes_in.at[g, b, part_rows(q)])
+
+            return 0
+
+        lax.fori_loop(0, steps, own_part, 0)
+
+        def store(b, value):
+            mass_sent[b:b + 1, :] = value
+
+        spread(store)
+
+        @pl.when(owner == 0)
+        def _():
+            mass_own[slot] = mass_sent[...]
+
+    for row in range(nr):
+        @pl.when(part_remote(row))
+        def _():
+            part_copy(row).start()
+
+    def own_spread(j):
+        def store(b, value):
+            mass_all[z, j * k + b:j * k + b + 1, :] = value
+
+        spread(store)
+
+    for j in range(m):
+        @pl.when((c * m + j > z) & (c * m + j < final))
+        def _():
+            for h in range(PIECES):
+                with scope("wait_down"):
+                    arrived(err_own.at[j, h * piece:(h + 1) * piece], own_recv.at[j, h])
+                count(
+                    err_own.at[j, h * piece:(h + 1) * piece],
+                    lambda b: codes.at[j * k + b, h * piece:(h + 1) * piece],
+                )
+            own_spread(j)
+
+    @pl.when(is_last)
+    def _():
+        j = m - 1
+        for h in range(PIECES):
+            at = slice(h * piece, (h + 1) * piece)
+            with scope("wait_last"):
+                for row in range(final):
+                    @pl.when(row != z)
+                    def _():
+                        arrived(last_in.at[row, h], last_recv.at[row, h])
+            total = delta[j, at]
+            for row in range(final):
+                total = total - last_in[row, h]
+            err_own[j, at] = dot3(total, w_high[...], w_low[...])
+            count(err_own.at[j, at], lambda b: codes.at[j * k + b, at])
+        own_spread(j)
 
     def mass_copy(row):
         return remote(mass_all.at[z], mass_all.at[z], mass_send.at[row], mass_recv.at[z], row, c)
@@ -361,6 +518,24 @@
         @pl.when(row != z)
         def _():
             mass_copy(row).start()
+
+    loss = jnp.zeros((8, rows), F32)
+    for j in reversed(range(m)):
+        @pl.when(c * m + j < z)
+        def _():
+            with scope("wait_up"):
+                for h in range(PIECES):
+                    arrived(err_own.at[j, h * piece:(h + 1) * piece], own_recv.at[j, h])
+
+        error = err_own[j]
+        errors_out[:, j * span:(j + 1) * span] = error
+        squared = error * error
+        loss = loss + lax.dot_general(
+            jnp.ones((8, span), F32), squared, (((1,), (1,)), ((), ())),
+            precision=lax.Precision.HIGHEST, preferred_element_type=F32,
+        )
+    loss_all[c, :, :rows] = loss
+
     for col in range(nc):
         @pl.when(col != c)
         def _():
@@ -371,20 +546,33 @@
         def _():
             delta_copy(j).wait_send()
 
+        @pl.when(code_sent(j))
+        def _():
+            code_copy(j).wait_send()
+
+    @pl.when((z == final) & is_last)
+    def _():
+        for row in range(final):
+            for i in range(k - 1):
+                tri_copy(row, i).wait_send()
+
     def drain(q, _):
+        g = group(q)
         for j in range(m):
-            @pl.when(c * m + j > z)
+            @pl.when((c * m + j > z) & (c * m + j < final))
             def _():
                 run_copy(q, j).wait_send()
 
-        @pl.when(is_owner)
-        def _():
-            for col in range(1, nc):
-                @pl.when(col > c)
-                def _():
-                    core_copy(q, col).wait_send()
-
-        @pl.when((is_owner & (q // PIECES < z)) | ((c == nc - 1) & (q // PIECES > z)))
+        @pl.when(is_last & (z < final) & (g != z))
+        def _():
+            last_copy(q).wait_send()
+
+        for col in range(nc):
+            @pl.when(is_owner & ((col > c) | ((col == 0) & (c > 0) & (g >= z))))
+            def _():
+                core_copy(q, col).wait_send()
+
+        @pl.when((is_owner & (g < z)) | (is_last & (z < final) & (g > z)))
         def _():
             own_copy(q).wait_send()
 
@@ -402,6 +590,7 @@
     for col in range(1, nc):
         loss_sum = loss_sum + loss_all[col, 0:1, :rows]
     loss_out[...] = loss_sum
+
     for row in range(nr):
         @pl.when(row != z)
         def _():
@@ -411,11 +600,23 @@
     for row in range(1, nr):
         mass_sum = mass_sum + mass_all[row]
     mass_out[...] = mass_sum
+    for j in range(m):
+        @pl.when(c * m + j < final)
+        def _():
+            @pl.when((c * m + j != z) | (c != 0))
+            def _():
+                with scope("wait_mass_part"):
+                    arrived(mass_own.at[j], part_recv.at[j])
+            mass_out[j * k:(j + 1) * k, :] = mass_out[j * k:(j + 1) * k, :] + mass_own[j]
 
     for row in range(nr):
         @pl.when(row != z)
         def _():
             mass_copy(row).wait_send()
+
+        @pl.when(part_remote(row))
+        def _():
+            part_copy(row).wait_send()
     for col in range(nc):
         @pl.when(col != c)
         def _():
@@ -440,13 +641,16 @@
     steps, piece = nr * PIECES, rows // PIECES
     blocks, code_count = codebook.shape[1], codebook.shape[3]
     block = inv_blocks.shape[2]
+    k = span // block
+    edges = max(k - 1, 1)
     dma = pltpu.SemaphoreType.DMA
     vmem = pl.BlockSpec(memory_space=pltpu.VMEM)
+    hbm = pl.BlockSpec(memory_space=pltpu.HBM)
     shapes = ((rows, width), (1, rows), (blocks, code_count))
     results = pl.pallas_call(
         functools.partial(kernel, nr, nc),
         out_shape=tuple(pltpu.VMEM(shape, F32) for shape in shapes),
-        in_specs=[pl.BlockSpec(memory_space=pltpu.HBM)] * 5,
+        in_specs=[hbm] * 5,
         out_specs=(vmem, vmem, vmem),
         scratch_shapes=[
             pltpu.VMEM(weights.shape[1:], F32),
@@ -457,22 +661,35 @@
             pltpu.VMEM((span, width), BF16),
             pltpu.VMEM((span, width), BF16),
             pltpu.VMEM((span, span), F32),
+            pltpu.VMEM((span, span), F32),
+            pltpu.VMEM((span, span), BF16),
+            pltpu.VMEM((span, span), BF16),
             pltpu.VMEM((span, span), BF16),
             pltpu.VMEM((span, span), BF16),
             pltpu.VMEM((m, rows, span), F32),
             pltpu.VMEM((blocks, rows, block), jnp.int32),
             pltpu.VMEM((nr, rows, span), F32),
+            pltpu.VMEM((nr, k, rows, block), jnp.int32),
             pltpu.VMEM((steps, m, piece, span), F32),
             pltpu.VMEM((steps, m, piece, span), F32),
+            pltpu.VMEM((nr, PIECES, piece, span), F32),
+            pltpu.VMEM((steps, piece, span), F32),
             pltpu.VMEM((steps, piece, span), F32),
             pltpu.VMEM((m, rows, span), F32),
+            pltpu.VMEM((k * 2 * (code_count // LOW), k * LOW), F32),
             pltpu.VMEM((nr, blocks, code_count), F32),
+            pltpu.VMEM((m, k, code_count), F32),
+            pltpu.VMEM((k, code_count), F32),
             pltpu.VMEM((nc, 8, max(rows, 128)), F32),
             dma((5,)),
             dma((m,)), dma((nr,)),
+            dma((m,)), dma((nr,)),
+            dma((nr, edges)), dma((edges,)),
             dma((steps, m)), dma((steps, m)),
+            dma((steps,)), dma((nr, PIECES)),
             dma((steps, nc)), dma((steps,)),
             dma((steps,)), dma((m, PIECES)),
+            dma((nr,)), dma((m,)),
             dma((nr,)), dma((nr,)),
             dma((nc,)), dma((nc,)),
         ],
@@ -486,7 +703,7 @@
         store,
         out_shape=tuple(jax.ShapeDtypeStruct(shape, F32) for shape in shapes),
         in_specs=[vmem] * 3,
-        out_specs=[pl.BlockSpec(memory_space=pltpu.HBM)] * 3,
+        out_specs=[hbm] * 3,
         scratch_shapes=[dma((3,))],
         compiler_params=pltpu.CompilerParams(vmem_limit_bytes=1024 * 1024),
     )(*results)

time: 45.7 us -> 41.3 us (0.904)
  Pallas kernels: 44.9 us -> 40.1 us
    pallas_call x1, Pallas kernels: 44.2 us -> 39.4 us  [local(): pl.pallas_call(functools.partial(kernel, nr, nc), out_shape=tuple((pltpu....]
where the time goes in v2:
time: 41.3 us; the launch traced here: 40.7 us
  Pallas kernels  40.1 us (97%)
  between operations  0.64 us (2%)
    pallas_call x1, Pallas kernels, local(): pl.pallas_call(functools.partial(kernel, nr, nc), out_shape=tuple((pltpu....  39.4 us

profile of v2, /device:TPU:1, one launch (start us, length us, event | category | flops | bytes accessed | tf_op | source)
XLA Modules:
  0.0 40.7 jit_solution(9536042567854453879)
XLA Ops:
  0.6 39.4 %shard_map.76 = (f32[64,1024]{1,0:T(8,128)S(1)}, f32[1,64]{1,0:T(1,128)S(1)}, f32[8,256]{1,0:T(8,128)S(1)}) custom-call(f32[64,1024]{1,0:T(8,128)} %bitcast.9, f32[8,2,256]{2,1,0:T(2,128)} %bitcast.11, s32[64,512]{1,0:T(8,128)} %bitcast.10, f32[8,128,128]{2,1,0:T(8,128)} %bitcast.8, f32[512,1024]{1,0:T(8,128)} %bitcast.7), custom_call_target="tpu_custom_call" | custom-call | tf_op jit(solution)/shard_map/pallas_call | solution.py:650
  40.0 0.7 %shard_map.77 = (f32[64,1024]{1,0:T(8,128)}, f32[1,64]{1,0:T(1,128)}, f32[8,256]{1,0:T(8,128)}) custom-call(f32[64,1024]{1,0:T(8,128)S(1)} %get-tuple-element.9.errors, f32[1,64]{1,0:T(1,128)S(1)} %get-tuple-element.10.loss, f32[8,256]{1,0:T(8,128)S(1)} %get-tuple-element.11.mass), custom_call_target="tpu_custom_call" | custom-call | tf_op jit(solution)/shard_map/pallas_call | solution.py:702

commit v3 on v2

--- a/solution.py
+++ b/solution.py
@@ -45,9 +45,10 @@
     errors_out, loss_out, mass_out,
     weights, codebook, assign, inverse, u_raw, u_high, u_low, triangle, v_full, v_high, v_low, w_high, w_low,
     delta, codes, delta_in, codes_in, run_in, run_out, last_in, last_out,
-    err_block, err_own, tally, mass_all, mass_own, mass_sent, loss_all,
+    err_block, err_own, err_zero, tally, mass_all, mass_own, mass_sent, loss_all,
     u_sem, d_send, d_recv, code_send, code_recv, tri_send, tri_recv, run_send, run_recv, last_send, last_recv,
-    core_send, core_recv, own_send, own_recv, part_send, part_recv, mass_send, mass_recv, loss_send, loss_recv,
+    core_send, core_recv, own_send, own_recv, zero_send, part_send, part_recv, mass_send, mass_recv,
+    loss_send, loss_recv, ready,
 ):
     z = lax.axis_index("row")
     c = lax.axis_index("col")
@@ -62,6 +63,8 @@
     steps = nr * PIECES
     piece = rows // PIECES
     final = nr - 1
+    pairs = span // 2
+    window = max(pairs, block)
     is_owner = (c == owner) & (z < final)
     is_last = c == nc - 1
 
@@ -87,14 +90,21 @@
     barrier = pltpu.get_barrier_semaphore()
     for step in range(1, nr * nc):
         other = lax.rem(z * nc + c + step, nr * nc)
-        pl.semaphore_signal(
-            barrier, inc=1, device_id={"row": other // nc, "col": other % nc},
-            device_id_type=pl.DeviceIdType.MESH,
-        )
+
+        @pl.when(z <= other // nc + 1)
+        def _():
+            pl.semaphore_signal(
+                barrier, inc=1, device_id={"row": other // nc, "col": other % nc},
+                device_id_type=pl.DeviceIdType.MESH,
+            )
 
     def enter():
         with scope("entry"):
-            pl.semaphore_wait(barrier, nr * nc - 1)
+            pl.semaphore_wait(barrier, (jnp.minimum(z + 1, nr - 1) + 1) * nc - 1)
+
+    def wait_ready():
+        with scope("wait_ready"):
+            pl.semaphore_wait(ready, (nr - 2 - z) * nc)
 
     def order(place):
         if nr < 3:
@@ -111,7 +121,10 @@
         return remote(delta.at[j], delta_in.at[z], d_send.at[j], d_recv.at[z], c * m + j, c)
 
     def code_copy(j):
-        return remote(codes.at[j * k:(j + 1) * k], codes_in.at[z], code_send.at[j], code_recv.at[z], c * m + j, 0)
+        low = j * pairs // window * window
+        return remote(
+            assign.at[:, low:low + window], codes_in.at[z], code_send.at[j], code_recv.at[z], c * m + j, 0
+        )
 
     def code_sent(j):
         return (c * m + j <= z) & (c * m + j < final) & ((c > 0) | (c * m + j < z))
@@ -127,9 +140,20 @@
     def run_copy(q, j):
         return remote(run_out.at[q, j], run_in.at[q, j], run_send.at[q, j], run_recv.at[q, j], z + 1, c)
 
+    def first(g):
+        return jnp.where(g == 0, 1, 0)
+
+    def solver(g):
+        return jnp.maximum(g, 1)
+
     def last_copy(q):
+        at = first(group(q)), z, q % PIECES
+        return remote(last_out.at[q], last_in.at[at], last_send.at[q], last_recv.at[at], solver(group(q)), c)
+
+    def zero_copy(h):
         return remote(
-            last_out.at[q], last_in.at[z, q % PIECES], last_send.at[q], last_recv.at[z, q % PIECES], group(q), c
+            err_zero.at[h], err_own.at[m - 1, h * piece:(h + 1) * piece],
+            zero_send.at[h], own_recv.at[m - 1, h], 0, c,
         )
 
     def core_copy(q, col):
@@ -147,9 +171,9 @@
 
     lane = lax.broadcasted_iota(jnp.int32, (rows, block), 1)
     for b in range(width // block):
-        first = b * (block // 2)
-        tile = first // block * block
-        code = take(assign[:, tile:tile + block], first - tile + lane // 2)
+        low = b * (block // 2)
+        tile = low // block * block
+        code = take(assign[:, tile:tile + block], low - tile + lane // 2)
         codes[b] = code
         inner = code % block
         value = jnp.zeros((rows, block), F32)
@@ -162,15 +186,23 @@
             value = jnp.where(code // block == part, both, value)
         j, at = b * block // span, b * block % span
         delta[j, :, at:at + block] = weights[:, b * block:(b + 1) * block] - value
-
-    @pl.when(z > 0)
-    def _():
-        enter()
-
-    for j in range(m):
-        @pl.when(c * m + j < z)
-        def _():
-            delta_copy(j).start()
+        if at + block == span:
+            if j == 0:
+                @pl.when(z > 0)
+                def _():
+                    enter()
+
+            @pl.when(c * m + j < z)
+            def _():
+                delta_copy(j).start()
+
+    for row in range(nr - 2):
+        for col in range(nc):
+            @pl.when(row + 1 < z)
+            def _():
+                pl.semaphore_signal(
+                    ready, inc=1, device_id={"row": row, "col": col}, device_id_type=pl.DeviceIdType.MESH,
+                )
 
     with scope("factor_loads"):
         for load in loads[3:]:
@@ -178,7 +210,7 @@
 
     @pl.when((z == final) & is_last)
     def _():
-        for row in reversed(range(final)):
+        for row in reversed(range(1, final)):
             for i in range(k - 1):
                 tri_copy(row, i).start()
 
@@ -242,9 +274,12 @@
 
         @pl.when((c == 0) & (z == j) & (z < final))
         def _():
-            codes_in[z] = codes[j * k:(j + 1) * k]
+            low = j * pairs // window * window
+            codes_in[z] = assign[:, low:low + window]
 
     late_core = (z == 0) & (c > owner)
+    relay_core = (z > 0) & (z < final) & (c > owner)
+    early_up = (z > 0) & (owner < nc - 1)
 
     def stage(q, _):
         g = group(q)
@@ -253,6 +288,10 @@
         @pl.when(is_last & (((z == final) & (q == 0)) | ((z == final - 1) & (q == PIECES))))
         def _():
             invert_last()
+
+        @pl.when((z > 0) & (z < nr - 2) & (q == (z + 1) * PIECES))
+        def _():
+            wait_ready()
 
         @pl.when(is_owner)
         def _():
@@ -290,7 +329,7 @@
                 def _():
                     core_copy(q, col).start()
 
-            @pl.when(g < z)
+            @pl.when((g < z) | ((g > z) & early_up))
             def _():
                 own_copy(q).start()
 
@@ -299,7 +338,28 @@
             with scope("wait_core"):
                 arrived(err_block.at[q], core_recv.at[q])
 
-        late = late_core & (q >= PIECES)
+        late = late_core & (q >= 2 * PIECES)
+        relay = relay_core & (q >= PIECES)
+        @pl.when(is_last & (z < final))
+        def _():
+            j = m - 1
+            change = dot3(
+                err_block[q], u_high[:, j * span:(j + 1) * span], u_low[:, j * span:(j + 1) * span]
+            )
+            change = change - jnp.where((g == 0) & (z == 0), delta[j, at], 0.0)
+
+            @pl.when(solver(g) == z)
+            def _():
+                last_in[first(g), z, q % PIECES] = change
+
+            @pl.when(solver(g) != z)
+            def _():
+                last_out[q] = change
+
+                @pl.when(jnp.logical_not(late))
+                def _():
+                    last_copy(q).start()
+
         for j in range(m):
             target = c * m + j
 
@@ -310,38 +370,23 @@
                 )
                 run_out[q, j] = jnp.where(g == z, delta[j, at], 0.0) - change
 
-                @pl.when(z > 0)
+                @pl.when((z > 0) & jnp.logical_not(relay))
                 def _():
                     with scope("wait_near_sum"):
                         arrived(run_in.at[q, j], run_recv.at[q, j])
                     run_out[q, j] = run_out[q, j] + run_in[q, j]
 
-                @pl.when(jnp.logical_not(late))
+                @pl.when(jnp.logical_not(late | relay))
                 def _():
                     run_copy(q, j).start()
 
-        @pl.when(is_last & (z < final))
-        def _():
-            j = m - 1
-            change = dot3(
-                err_block[q], u_high[:, j * span:(j + 1) * span], u_low[:, j * span:(j + 1) * span]
-            )
-
-            @pl.when(g == z)
-            def _():
-                last_in[z, q % PIECES] = change
-
-            @pl.when(g != z)
-            def _():
-                last_out[q] = change
-
-                @pl.when(jnp.logical_not(late))
-                def _():
-                    last_copy(q).start()
-
         return 0
 
     lax.fori_loop(0, steps, stage, 0)
+
+    @pl.when((z == 0) & (nr > 2))
+    def _():
+        wait_ready()
 
     for j in range(m):
         @pl.when(late_core & (c * m + j < final))
@@ -350,6 +395,17 @@
                 run_copy(q, j).start()
                 return 0
 
+            lax.fori_loop(2 * PIECES, steps, release, 0)
+
+        @pl.when(relay_core & (c * m + j < final))
+        def _():
+            def release(q, _):
+                with scope("wait_far_sum"):
+                    arrived(run_in.at[q, j], run_recv.at[q, j])
+                run_out[q, j] = run_out[q, j] + run_in[q, j]
+                run_copy(q, j).start()
+                return 0
+
             lax.fori_loop(PIECES, steps, release, 0)
 
     @pl.when(late_core & is_last)
@@ -358,9 +414,9 @@
             last_copy(steps - 1 - i).start()
             return 0
 
-        lax.fori_loop(0, steps - PIECES, release, 0)
-
-    @pl.when(is_last & (z < final))
+        lax.fori_loop(0, steps - 2 * PIECES, release, 0)
+
+    @pl.when(is_last & (z < final) & jnp.logical_not(early_up))
     def _():
         def upward(i, _):
             q = steps - 1 - i
@@ -373,9 +429,28 @@
 
         lax.fori_loop(0, steps, upward, 0)
 
-    @pl.when(is_last & (z < final - 1))
+    @pl.when(is_last & (z > 0) & (z < final - 1))
     def _():
         invert_last()
+
+    def solved(which, h):
+        with scope("wait_last"):
+            for row in range(final):
+                @pl.when(row != z)
+                def _():
+                    arrived(last_in.at[which, row, h], last_recv.at[which, row, h])
+        total = -last_in[which, 0, h]
+        for row in range(1, final):
+            total = total - last_in[which, row, h]
+        if which == 0:
+            total = total + delta[m - 1, h * piece:(h + 1) * piece]
+        return dot3(total, w_high[...], w_low[...])
+
+    @pl.when(is_last & (z == 1))
+    def _():
+        for h in range(PIECES):
+            err_zero[h] = solved(1, h)
+            zero_copy(h).start()
 
     high_count = code_count // LOW
     fold = 2 * high_count
@@ -388,7 +463,7 @@
             iota_low = lax.broadcasted_iota(jnp.int32, (LOW, block), 0)
             left, right = [], []
             for b in range(k):
-                code = code_at(b)[at, :]
+                code = code_at(b, at)
                 value = error_at[at, b * block:(b + 1) * block]
                 value = value * value
                 coarse = value.astype(BF16).astype(F32)
@@ -453,7 +528,15 @@
                     def _():
                         arrived(codes_in.at[g], code_recv.at[g])
 
-                count(err_block.at[q], lambda b: codes_in.at[g, b, part_rows(q)])
+                shift = 0 if window == pairs else lax.rem(slot * pairs, window)
+
+                def code_at(b, at):
+                    low = b * (block // 2)
+                    tile = low // block * block
+                    source = codes_in[g, pl.ds(q % PIECES * piece + at.start, chunk), tile:tile + block]
+                    return take(source, shift + low - tile + lane[:chunk] // 2)
+
+                count(err_block.at[q], code_at)
 
             return 0
 
@@ -480,32 +563,26 @@
         spread(store)
 
     for j in range(m):
-        @pl.when((c * m + j > z) & (c * m + j < final))
+        @pl.when((c * m + j > z) & ((c * m + j < final) | (z == 0)))
         def _():
             for h in range(PIECES):
                 with scope("wait_down"):
                     arrived(err_own.at[j, h * piece:(h + 1) * piece], own_recv.at[j, h])
                 count(
                     err_own.at[j, h * piece:(h + 1) * piece],
-                    lambda b: codes.at[j * k + b, h * piece:(h + 1) * piece],
+                    lambda b, at: codes[j * k + b, pl.ds(h * piece + at.start, chunk), :],
                 )
             own_spread(j)
 
-    @pl.when(is_last)
+    @pl.when(is_last & (z > 0))
     def _():
         j = m - 1
         for h in range(PIECES):
-            at = slice(h * piece, (h + 1) * piece)
-            with scope("wait_last"):
-                for row in range(final):
-                    @pl.when(row != z)
-                    def _():
-                        arrived(last_in.at[row, h], last_recv.at[row, h])
-            total = delta[j, at]
-            for row in range(final):
-                total = total - last_in[row, h]
-            err_own[j, at] = dot3(total, w_high[...], w_low[...])
-            count(err_own.at[j, at], lambda b: codes.at[j * k + b, at])
+            err_own[j, h * piece:(h + 1) * piece] = solved(0, h)
+            count(
+                err_own.at[j, h * piece:(h + 1) * piece],
+                lambda b, at: codes[j * k + b, pl.ds(h * piece + at.start, chunk), :],
+            )
         own_spread(j)
 
     def mass_copy(row):
@@ -552,7 +629,7 @@
 
     @pl.when((z == final) & is_last)
     def _():
-        for row in range(final):
+        for row in range(1, final):
             for i in range(k - 1):
                 tri_copy(row, i).wait_send()
 
@@ -563,7 +640,7 @@
             def _():
                 run_copy(q, j).wait_send()
 
-        @pl.when(is_last & (z < final) & (g != z))
+        @pl.when(is_last & (z < final) & (solver(g) != z))
         def _():
             last_copy(q).wait_send()
 
@@ -572,7 +649,9 @@
             def _():
                 core_copy(q, col).wait_send()
 
-        @pl.when((is_owner & (g < z)) | (is_last & (z < final) & (g > z)))
+        down = is_owner & ((g < z) | ((g > z) & early_up))
+
+        @pl.when(down | (is_last & (z < final) & (g > z) & jnp.logical_not(early_up)))
         def _():
             own_copy(q).wait_send()
 
@@ -580,6 +659,11 @@
 
     with scope("drain"):
         lax.fori_loop(0, steps, drain, 0)
+
+    @pl.when(is_last & (z == 1))
+    def _():
+        for h in range(PIECES):
+            zero_copy(h).wait_send()
 
     for col in range(nc):
         @pl.when(col != c)
@@ -669,13 +753,14 @@
             pltpu.VMEM((m, rows, span), F32),
             pltpu.VMEM((blocks, rows, block), jnp.int32),
             pltpu.VMEM((nr, rows, span), F32),
-            pltpu.VMEM((nr, k, rows, block), jnp.int32),
+            pltpu.VMEM((nr, rows, max(span // 2, block)), jnp.int32),
             pltpu.VMEM((steps, m, piece, span), F32),
             pltpu.VMEM((steps, m, piece, span), F32),
-            pltpu.VMEM((nr, PIECES, piece, span), F32),
+            pltpu.VMEM((2, nr, PIECES, piece, span), F32),
             pltpu.VMEM((steps, piece, span), F32),
             pltpu.VMEM((steps, piece, span), F32),
             pltpu.VMEM((m, rows, span), F32),
+            pltpu.VMEM((PIECES, piece, span), F32),
             pltpu.VMEM((k * 2 * (code_count // LOW), k * LOW), F32),
             pltpu.VMEM((nr, blocks, code_count), F32),
             pltpu.VMEM((m, k, code_count), F32),
@@ -686,12 +771,12 @@
             dma((m,)), dma((nr,)),
             dma((nr, edges)), dma((edges,)),
             dma((steps, m)), dma((steps, m)),
-            dma((steps,)), dma((nr, PIECES)),
+            dma((steps,)), dma((2, nr, PIECES)),
             dma((steps, nc)), dma((steps,)),
-            dma((steps,)), dma((m, PIECES)),
+            dma((steps,)), dma((m, PIECES)), dma((PIECES,)),
             dma((nr,)), dma((m,)),
             dma((nr,)), dma((nr,)),
-            dma((nc,)), dma((nc,)),
+            dma((nc,)), dma((nc,)), pltpu.SemaphoreType.REGULAR,
         ],
         compiler_params=pltpu.CompilerParams(
             collective_id=0, has_side_effects=True, vmem_limit_bytes=40 * 1024 * 1024

time: 41.3 us -> 43.6 us (1.056)
  Pallas kernels: 40.1 us -> 42.7 us
    pallas_call x1, Pallas kernels: 39.4 us -> 42 us  [local(): pl.pallas_call(functools.partial(kernel, nr, nc), out_shape=tuple((pltpu....]
where the time goes in v3:
time: 43.6 us; the launch traced here: 43.4 us
  Pallas kernels  42.7 us (98%)
  between operations  0.64 us (1%)
    pallas_call x1, Pallas kernels, local(): pl.pallas_call(functools.partial(kernel, nr, nc), out_shape=tuple((pltpu....  42 us

profile of v3, /device:TPU:1, one launch (start us, length us, event | category | flops | bytes accessed | tf_op | source)
XLA Modules:
  0.0 43.4 jit_solution(7280377492698468367)
XLA Ops:
  0.6 42.0 %shard_map.76 = (f32[64,1024]{1,0:T(8,128)S(1)}, f32[1,64]{1,0:T(1,128)S(1)}, f32[8,256]{1,0:T(8,128)S(1)}) custom-call(f32[64,1024]{1,0:T(8,128)} %bitcast.9, f32[8,2,256]{2,1,0:T(2,128)} %bitcast.11, s32[64,512]{1,0:T(8,128)} %bitcast.10, f32[8,128,128]{2,1,0:T(8,128)} %bitcast.8, f32[512,1024]{1,0:T(8,128)} %bitcast.7), custom_call_target="tpu_custom_call" | custom-call | tf_op jit(solution)/shard_map/pallas_call | solution.py:734
  42.6 0.7 %shard_map.77 = (f32[64,1024]{1,0:T(8,128)}, f32[1,64]{1,0:T(1,128)}, f32[8,256]{1,0:T(8,128)}) custom-call(f32[64,1024]{1,0:T(8,128)S(1)} %get-tuple-element.9.errors, f32[1,64]{1,0:T(1,128)S(1)} %get-tuple-element.10.loss, f32[8,256]{1,0:T(8,128)S(1)} %get-tuple-element.11.mass), custom_call_target="tpu_custom_call" | custom-call | tf_op jit(solution)/shard_map/pallas_call | solution.py:787

commit v4 on v3

--- a/solution.py
+++ b/solution.py
@@ -44,9 +44,9 @@
     weights_hbm, codebook_hbm, assign_hbm, inverse_hbm, factor,
     errors_out, loss_out, mass_out,
     weights, codebook, assign, inverse, u_raw, u_high, u_low, triangle, v_full, v_high, v_low, w_high, w_low,
-    delta, codes, delta_in, codes_in, run_in, run_out, last_in, last_out,
+    delta, codes, delta_in, codes_in, run_in, run_out, last_in, last_out, zero_in,
     err_block, err_own, err_zero, tally, mass_all, mass_own, mass_sent, loss_all,
-    u_sem, d_send, d_recv, code_send, code_recv, tri_send, tri_recv, run_send, run_recv, last_send, last_recv,
+    u_sem, d_send, d_recv, code_send, code_recv, tri_send, tri_recv, run_send, run_recv, last_send, last_recv, zero_recv,
     core_send, core_recv, own_send, own_recv, zero_send, part_send, part_recv, mass_send, mass_recv,
     loss_send, loss_recv, ready,
 ):
@@ -114,11 +114,27 @@
     def group(q):
         return order(q // PIECES)
 
+    def farthest(i):
+        return order(nr - 1 - i // PIECES) * PIECES + i % PIECES
+
+    def nearest(i):
+        return order(i // PIECES) * PIECES + i % PIECES
+
     def part_rows(q):
         return pl.ds(pl.multiple_of(q % PIECES * piece, piece), piece)
 
-    def delta_copy(j):
-        return remote(delta.at[j], delta_in.at[z], d_send.at[j], d_recv.at[z], c * m + j, c)
+    def delta_copy(j, h):
+        at = slice(h * piece, (h + 1) * piece)
+        return remote(delta.at[j, at], delta_in.at[z, at], d_send.at[j, h], d_recv.at[z, h], c * m + j, c)
+
+    def send_delta(j, when):
+        @pl.when((c * m + j < z) & when)
+        def _():
+            for h in range(PIECES):
+                delta_copy(j, h).start()
+
+    def urgent(j):
+        return (c * m + j == 0) & (z != nr - 2)
 
     def code_copy(j):
         low = j * pairs // window * window
@@ -149,6 +165,9 @@
     def last_copy(q):
         at = first(group(q)), z, q % PIECES
         return remote(last_out.at[q], last_in.at[at], last_send.at[q], last_recv.at[at], solver(group(q)), c)
+
+    def zero_sum(q):
+        return remote(last_out.at[q], zero_in.at[q], last_send.at[q], zero_recv.at[q], 1, c)
 
     def zero_copy(h):
         return remote(
@@ -192,9 +211,7 @@
                 def _():
                     enter()
 
-            @pl.when(c * m + j < z)
-            def _():
-                delta_copy(j).start()
+            send_delta(j, urgent(j))
 
     for row in range(nr - 2):
         for col in range(nc):
@@ -268,6 +285,9 @@
         enter()
 
     for j in range(m):
+        send_delta(j, jnp.logical_not(urgent(j)))
+
+    for j in range(m):
         @pl.when(code_sent(j))
         def _():
             code_copy(j).start()
@@ -279,7 +299,13 @@
 
     late_core = (z == 0) & (c > owner)
     relay_core = (z > 0) & (z < final) & (c > owner)
-    early_up = (z > 0) & (owner < nc - 1)
+    early_up = z < 0
+
+    def forward(q, j):
+        with scope("wait_far_sum"):
+            arrived(run_in.at[q, j], run_recv.at[q, j])
+        run_out[q, j] = run_out[q, j] + run_in[q, j]
+        run_copy(q, j).start()
 
     def stage(q, _):
         g = group(q)
@@ -306,10 +332,8 @@
 
             @pl.when(g > z)
             def _():
-                @pl.when(q % PIECES == 0)
-                def _():
-                    with scope("wait_delta"):
-                        arrived(delta_in.at[g], d_recv.at[g])
+                with scope("wait_delta"):
+                    arrived(delta_in.at[g, at], d_recv.at[g, q % PIECES])
 
                 run_in[q, slot] = run_in[q, slot] + delta_in[g, at]
 
@@ -348,17 +372,21 @@
             )
             change = change - jnp.where((g == 0) & (z == 0), delta[j, at], 0.0)
 
-            @pl.when(solver(g) == z)
+            @pl.when((z <= 1) | (solver(g) != z))
+            def _():
+                last_out[q] = change
+
+            @pl.when((z > 1) & (solver(g) == z))
             def _():
                 last_in[first(g), z, q % PIECES] = change
 
-            @pl.when(solver(g) != z)
-            def _():
-                last_out[q] = change
-
-                @pl.when(jnp.logical_not(late))
-                def _():
-                    last_copy(q).start()
+            @pl.when((z == 0) & (q < PIECES))
+            def _():
+                zero_sum(q).start()
+
+            @pl.when((z > 1) & (solver(g) != z))
+            def _():
+                last_copy(q).start()
 
         for j in range(m):
             target = c * m + j
@@ -380,6 +408,10 @@
                 def _():
                     run_copy(q, j).start()
 
+                @pl.when(relay & (q >= 2 * PIECES))
+                def _():
+                    forward(q - PIECES, j)
+
         return 0
 
     lax.fori_loop(0, steps, stage, 0)
@@ -400,34 +432,33 @@
         @pl.when(relay_core & (c * m + j < final))
         def _():
             def release(q, _):
-                with scope("wait_far_sum"):
-                    arrived(run_in.at[q, j], run_recv.at[q, j])
-                run_out[q, j] = run_out[q, j] + run_in[q, j]
-                run_copy(q, j).start()
+                forward(q, j)
                 return 0
 
-            lax.fori_loop(PIECES, steps, release, 0)
+            lax.fori_loop(steps - PIECES, steps, release, 0)
 
     @pl.when(late_core & is_last)
     def _():
         def release(i, _):
-            last_copy(steps - 1 - i).start()
+            zero_sum(farthest(i)).start()
             return 0
 
-        lax.fori_loop(0, steps - 2 * PIECES, release, 0)
-
-    @pl.when(is_last & (z < final) & jnp.logical_not(early_up))
-    def _():
-        def upward(i, _):
-            q = steps - 1 - i
-
-            @pl.when(group(q) > z)
-            def _():
-                own_copy(q).start()
-
+        lax.fori_loop(0, steps - PIECES, release, 0)
+
+    def joined(q):
+        with scope("wait_zero"):
+            arrived(zero_in.at[q], zero_recv.at[q])
+        return last_out[q] + zero_in[q]
+
+    @pl.when(is_last & (z == 1) & (z < final))
+    def _():
+        def relayed(i, _):
+            q = farthest(i)
+            last_out[q] = joined(q)
+            last_copy(q).start()
             return 0
 
-        lax.fori_loop(0, steps, upward, 0)
+        lax.fori_loop(0, steps - 2 * PIECES, relayed, 0)
 
     @pl.when(is_last & (z > 0) & (z < final - 1))
     def _():
@@ -435,12 +466,12 @@
 
     def solved(which, h):
         with scope("wait_last"):
-            for row in range(final):
+            for row in range(1, final):
                 @pl.when(row != z)
                 def _():
                     arrived(last_in.at[which, row, h], last_recv.at[which, row, h])
-        total = -last_in[which, 0, h]
-        for row in range(1, final):
+        total = -last_in[which, 1, h]
+        for row in range(2, final):
             total = total - last_in[which, row, h]
         if which == 0:
             total = total + delta[m - 1, h * piece:(h + 1) * piece]
@@ -449,8 +480,24 @@
     @pl.when(is_last & (z == 1))
     def _():
         for h in range(PIECES):
+            last_in[1, 1, h] = joined(h)
             err_zero[h] = solved(1, h)
             zero_copy(h).start()
+        for h in range(PIECES):
+            last_in[0, 1, h] = joined(PIECES + h)
+
+    @pl.when(is_last & (z < final) & jnp.logical_not(early_up))
+    def _():
+        def upward(i, _):
+            q = nearest(i)
+
+            @pl.when(group(q) > z)
+            def _():
+                own_copy(q).start()
+
+            return 0
+
+        lax.fori_loop(0, steps, upward, 0)
 
     high_count = code_count // LOW
     fold = 2 * high_count
@@ -483,23 +530,18 @@
                 (((1,), (1,)), ((), ())), preferred_element_type=F32,
             )
 
-        total = lax.fori_loop(0, piece // chunk, gather, jnp.zeros(tally.shape, F32), unroll=4)
-        tally[...] = tally[...] + total
+        total = lax.fori_loop(0, piece // chunk, gather, jnp.zeros((k * fold, k * LOW), F32), unroll=4)
+        tally[:, :k * LOW] = tally[:, :k * LOW] + total
 
     def spread(store):
-        total = tally[...]
-        row_id = lax.broadcasted_iota(jnp.int32, total.shape, 0)
-        col_id = lax.broadcasted_iota(jnp.int32, total.shape, 1)
-        total = jnp.where(row_id // fold == col_id // LOW, total, 0.0)
-        wide_row = lax.broadcasted_iota(jnp.int32, (k * LOW, code_count), 0)
-        wide_col = lax.broadcasted_iota(jnp.int32, (k * LOW, code_count), 1)
-        wide = jnp.where(wide_row % LOW == wide_col % LOW, 1.0, 0.0)
-        wide = jnp.dot(total, wide, precision=lax.Precision.HIGHEST, preferred_element_type=F32)
-        out_row = lax.broadcasted_iota(jnp.int32, wide.shape, 0)
-        out_col = lax.broadcasted_iota(jnp.int32, wide.shape, 1)
-        wide = jnp.where(out_row % high_count == out_col // LOW, wide, 0.0)
+        spot = lax.broadcasted_iota(jnp.int32, (high_count, block), 1)
+        level = lax.broadcasted_iota(jnp.int32, (high_count, block), 0)
         for b in range(k):
-            store(b, jnp.sum(wide[b * fold:(b + 1) * fold], axis=0, keepdims=True))
+            total = tally[b * fold:b * fold + high_count] + tally[b * fold + high_count:(b + 1) * fold]
+            total = take(total, b * LOW + spot % LOW)
+            for part in range(code_count // block):
+                mine = level == part * (block // LOW) + spot // LOW
+                store(b, part, jnp.sum(jnp.where(mine, total, 0.0), axis=0, keepdims=True))
         tally[...] = jnp.zeros_like(tally)
 
     tally[...] = jnp.zeros_like(tally)
@@ -542,8 +584,8 @@
 
         lax.fori_loop(0, steps, own_part, 0)
 
-        def store(b, value):
-            mass_sent[b:b + 1, :] = value
+        def store(b, part, value):
+            mass_sent[b:b + 1, part * block:(part + 1) * block] = value
 
         spread(store)
 
@@ -557,8 +599,8 @@
             part_copy(row).start()
 
     def own_spread(j):
-        def store(b, value):
-            mass_all[z, j * k + b:j * k + b + 1, :] = value
+        def store(b, part, value):
+            mass_all[z, j * k + b:j * k + b + 1, part * block:(part + 1) * block] = value
 
         spread(store)
 
@@ -621,7 +663,8 @@
     for j in range(m):
         @pl.when(c * m + j < z)
         def _():
-            delta_copy(j).wait_send()
+            for h in range(PIECES):
+                delta_copy(j, h).wait_send()
 
         @pl.when(code_sent(j))
         def _():
@@ -640,7 +683,11 @@
             def _():
                 run_copy(q, j).wait_send()
 
-        @pl.when(is_last & (z < final) & (solver(g) != z))
+        @pl.when(is_last & (z == 0))
+        def _():
+            zero_sum(q).wait_send()
+
+        @pl.when(is_last & (z > 0) & (z < final) & (solver(g) != z))
         def _():
             last_copy(q).wait_send()
 
@@ -759,19 +806,20 @@
             pltpu.VMEM((2, nr, PIECES, piece, span), F32),
             pltpu.VMEM((steps, piece, span), F32),
             pltpu.VMEM((steps, piece, span), F32),
+            pltpu.VMEM((steps, piece, span), F32),
             pltpu.VMEM((m, rows, span), F32),
             pltpu.VMEM((PIECES, piece, span), F32),
-            pltpu.VMEM((k * 2 * (code_count // LOW), k * LOW), F32),
+            pltpu.VMEM((k * 2 * (code_count // LOW), block), F32),
             pltpu.VMEM((nr, blocks, code_count), F32),
             pltpu.VMEM((m, k, code_count), F32),
             pltpu.VMEM((k, code_count), F32),
             pltpu.VMEM((nc, 8, max(rows, 128)), F32),
             dma((5,)),
-            dma((m,)), dma((nr,)),
+            dma((m, PIECES)), dma((nr, PIECES)),
             dma((m,)), dma((nr,)),
             dma((nr, edges)), dma((edges,)),
             dma((steps, m)), dma((steps, m)),
-            dma((steps,)), dma((2, nr, PIECES)),
+            dma((steps,)), dma((2, nr, PIECES)), dma((steps,)),
             dma((steps, nc)), dma((steps,)),
             dma((steps,)), dma((m, PIECES)), dma((PIECES,)),
             dma((nr,)), dma((m,)),

time: 43.6 us -> 35.9 us (0.82)
  the two profiles are of different devices: /device:TPU:1 before, /device:TPU:29 now
where the time goes in v4:
time: 35.9 us; the launch traced here: 35.8 us
  Pallas kernels  35.1 us (98%)
  between operations  0.64 us (2%)
    pallas_call x1, Pallas kernels, local(): pl.pallas_call(functools.partial(kernel, nr, nc), out_shape=tuple((pltpu....  34.4 us
    pallas_call x1, Pallas kernels, local(): pl.pallas_call(store, out_shape=tuple((jax.ShapeDtypeStruct(shape, F32) f...  0.74 us

profile of v4, /device:TPU:29, one launch (start us, length us, event | category | flops | bytes accessed | tf_op | source)
XLA Modules:
  0.0 35.8 jit_solution(14734527301812406802)
XLA Ops:
  0.6 34.4 %shard_map.76 = (f32[64,1024]{1,0:T(8,128)S(1)}, f32[1,64]{1,0:T(1,128)S(1)}, f32[8,256]{1,0:T(8,128)S(1)}) custom-call(f32[64,1024]{1,0:T(8,128)} %bitcast.9, f32[8,2,256]{2,1,0:T(2,128)} %bitcast.11, s32[64,512]{1,0:T(8,128)} %bitcast.10, f32[8,128,128]{2,1,0:T(8,128)} %bitcast.8, f32[512,1024]{1,0:T(8,128)} %bitcast.7), custom_call_target="tpu_custom_call" | custom-call | tf_op jit(solution)/shard_map/pallas_call | solution.py:781
  35.0 0.7 %shard_map.77 = (f32[64,1024]{1,0:T(8,128)}, f32[1,64]{1,0:T(1,128)}, f32[8,256]{1,0:T(8,128)}) custom-call(f32[64,1024]{1,0:T(8,128)S(1)} %get-tuple-element.9.errors, f32[1,64]{1,0:T(1,128)S(1)} %get-tuple-element.10.loss, f32[8,256]{1,0:T(8,128)S(1)} %get-tuple-element.11.mass), custom_call_target="tpu_custom_call" | custom-call | tf_op jit(solution)/shard_map/pallas_call | solution.py:835

commit v5 on v4

--- a/solution.py
+++ b/solution.py
@@ -45,10 +45,10 @@
     errors_out, loss_out, mass_out,
     weights, codebook, assign, inverse, u_raw, u_high, u_low, triangle, v_full, v_high, v_low, w_high, w_low,
     delta, codes, delta_in, codes_in, run_in, run_out, last_in, last_out, zero_in,
-    err_block, err_own, err_zero, tally, mass_all, mass_own, mass_sent, loss_all,
+    err_block, err_own, err_zero, tally, mass_all, mass_own, mass_sent, loss_all, loss_up, loss_in,
     u_sem, d_send, d_recv, code_send, code_recv, tri_send, tri_recv, run_send, run_recv, last_send, last_recv, zero_recv,
     core_send, core_recv, own_send, own_recv, zero_send, part_send, part_recv, mass_send, mass_recv,
-    loss_send, loss_recv, ready,
+    loss_send, loss_recv, up_send, up_recv, ready,
 ):
     z = lax.axis_index("row")
     c = lax.axis_index("col")
@@ -114,8 +114,15 @@
     def group(q):
         return order(q // PIECES)
 
+    def early_up(g):
+        return (z > 0) & (owner < nc - 1) & (g == nr)
+
     def farthest(i):
         return order(nr - 1 - i // PIECES) * PIECES + i % PIECES
+
+    def zero_order(i):
+        turn = i // PIECES
+        return farthest(jnp.where(turn == nr - 2, i + PIECES, jnp.where(turn == nr - 1, i - PIECES, i)))
 
     def nearest(i):
         return order(i // PIECES) * PIECES + i % PIECES
@@ -189,29 +196,32 @@
             load.wait()
 
     lane = lax.broadcasted_iota(jnp.int32, (rows, block), 1)
-    for b in range(width // block):
-        low = b * (block // 2)
-        tile = low // block * block
-        code = take(assign[:, tile:tile + block], low - tile + lane // 2)
-        codes[b] = code
-        inner = code % block
-        value = jnp.zeros((rows, block), F32)
-        for part in range(code_count // block):
-            picked = []
-            for comp in range(2):
-                table = codebook[b, comp:comp + 1, part * block:(part + 1) * block]
-                picked.append(take(jnp.broadcast_to(table, (rows, block)), inner))
-            both = jnp.where(lane % 2 == 0, picked[0], picked[1])
-            value = jnp.where(code // block == part, both, value)
-        j, at = b * block // span, b * block % span
-        delta[j, :, at:at + block] = weights[:, b * block:(b + 1) * block] - value
-        if at + block == span:
-            if j == 0:
-                @pl.when(z > 0)
-                def _():
-                    enter()
-
-            send_delta(j, urgent(j))
+
+    def subtract(j):
+        for b in range(j * k, (j + 1) * k):
+            low = b * (block // 2)
+            tile = low // block * block
+            code = take(assign[:, tile:tile + block], low - tile + lane // 2)
+            codes[b] = code
+            inner = code % block
+            value = jnp.zeros((rows, block), F32)
+            for part in range(code_count // block):
+                picked = []
+                for comp in range(2):
+                    table = codebook[b, comp:comp + 1, part * block:(part + 1) * block]
+                    picked.append(take(jnp.broadcast_to(table, (rows, block)), inner))
+                both = jnp.where(lane % 2 == 0, picked[0], picked[1])
+                value = jnp.where(code // block == part, both, value)
+            at = (b - j * k) * block
+            delta[j, :, at:at + block] = weights[:, b * block:(b + 1) * block] - value
+
+    subtract(0)
+
+    @pl.when(z > 0)
+    def _():
+        enter()
+
+    send_delta(0, urgent(0))
 
     for row in range(nr - 2):
         for col in range(nc):
@@ -224,6 +234,10 @@
     with scope("factor_loads"):
         for load in loads[3:]:
             load.wait()
+
+    def rest():
+        for j in range(1, m):
+            subtract(j)
 
     @pl.when((z == final) & is_last)
     def _():
@@ -250,6 +264,7 @@
 
     @pl.when(is_owner)
     def _():
+        rest()
         base = slot * span
         high, low = inverted(slot * k, lambda top, middle, end: u_raw[
             top:middle, pl.ds(pl.multiple_of(base + middle, block), end - middle)
@@ -257,6 +272,10 @@
         v_high[...] = high
         v_low[...] = low
 
+    @pl.when(jnp.logical_not(is_owner))
+    def _():
+        rest()
+
     for j in range(m):
         @pl.when(c * m + j > z)
         def _():
@@ -299,7 +318,6 @@
 
     late_core = (z == 0) & (c > owner)
     relay_core = (z > 0) & (z < final) & (c > owner)
-    early_up = z < 0
 
     def forward(q, j):
         with scope("wait_far_sum"):
@@ -353,7 +371,7 @@
                 def _():
                     core_copy(q, col).start()
 
-            @pl.when((g < z) | ((g > z) & early_up))
+            @pl.when((g < z) | ((g > z) & early_up(g)))
             def _():
                 own_copy(q).start()
 
@@ -363,7 +381,6 @@
                 arrived(err_block.at[q], core_recv.at[q])
 
         late = late_core & (q >= 2 * PIECES)
-        relay = relay_core & (q >= PIECES)
         @pl.when(is_last & (z < final))
         def _():
             j = m - 1
@@ -380,10 +397,6 @@
             def _():
                 last_in[first(g), z, q % PIECES] = change
 
-            @pl.when((z == 0) & (q < PIECES))
-            def _():
-                zero_sum(q).start()
-
             @pl.when((z > 1) & (solver(g) != z))
             def _():
                 last_copy(q).start()
@@ -398,17 +411,17 @@
                 )
                 run_out[q, j] = jnp.where(g == z, delta[j, at], 0.0) - change
 
-                @pl.when((z > 0) & jnp.logical_not(relay))
+                @pl.when((z > 0) & jnp.logical_not(relay_core))
                 def _():
                     with scope("wait_near_sum"):
                         arrived(run_in.at[q, j], run_recv.at[q, j])
                     run_out[q, j] = run_out[q, j] + run_in[q, j]
 
-                @pl.when(jnp.logical_not(late | relay))
+                @pl.when(jnp.logical_not(late | relay_core))
                 def _():
                     run_copy(q, j).start()
 
-                @pl.when(relay & (q >= 2 * PIECES))
+                @pl.when(relay_core & (q >= PIECES))
                 def _():
                     forward(q - PIECES, j)
 
@@ -440,10 +453,10 @@
     @pl.when(late_core & is_last)
     def _():
         def release(i, _):
-            zero_sum(farthest(i)).start()
+            zero_sum(zero_order(i)).start()
             return 0
 
-        lax.fori_loop(0, steps - PIECES, release, 0)
+        lax.fori_loop(0, steps, release, 0)
 
     def joined(q):
         with scope("wait_zero"):
@@ -486,22 +499,26 @@
         for h in range(PIECES):
             last_in[0, 1, h] = joined(PIECES + h)
 
-    @pl.when(is_last & (z < final) & jnp.logical_not(early_up))
-    def _():
+    def send_up():
         def upward(i, _):
             q = nearest(i)
 
-            @pl.when(group(q) > z)
+            @pl.when((group(q) > z) & jnp.logical_not(early_up(group(q))))
             def _():
                 own_copy(q).start()
 
             return 0
 
         lax.fori_loop(0, steps, upward, 0)
+
+    @pl.when(is_last & (z > 0) & (z < final))
+    def _():
+        send_up()
 
     high_count = code_count // LOW
     fold = 2 * high_count
-    chunk = 8
+    chunk = 16
+    half = chunk // 2
 
     def count(error_at, code_at):
         def gather(step, total):
@@ -509,15 +526,19 @@
             iota_high = lax.broadcasted_iota(jnp.int32, (high_count, block), 0)
             iota_low = lax.broadcasted_iota(jnp.int32, (LOW, block), 0)
             left, right = [], []
+            even = lax.broadcasted_iota(jnp.int32, (half, block), 1) % 2 == 0
             for b in range(k):
                 code = code_at(b, at)
+                code = jnp.where(even, code[:half], code[half:])
                 value = error_at[at, b * block:(b + 1) * block]
                 value = value * value
+                upper, lower = value[:half], value[half:]
+                value = jnp.where(even, upper + pltpu.roll(upper, block - 1, 1), lower + pltpu.roll(lower, 1, 1))
                 coarse = value.astype(BF16).astype(F32)
                 fine = value - coarse
                 code_high, code_low = code // LOW, code % LOW
                 top, bottom, marks = [], [], []
-                for r in range(chunk):
+                for r in range(half):
                     hit = jnp.broadcast_to(code_high[r:r + 1], (high_count, block)) == iota_high
                     top.append(jnp.where(hit, jnp.broadcast_to(coarse[r:r + 1], (high_count, block)), 0.0).astype(BF16))
                     bottom.append(jnp.where(hit, jnp.broadcast_to(fine[r:r + 1], (high_count, block)), 0.0).astype(BF16))
@@ -530,7 +551,7 @@
                 (((1,), (1,)), ((), ())), preferred_element_type=F32,
             )
 
-        total = lax.fori_loop(0, piece // chunk, gather, jnp.zeros((k * fold, k * LOW), F32), unroll=4)
+        total = lax.fori_loop(0, piece // chunk, gather, jnp.zeros((k * fold, k * LOW), F32), unroll=2)
         tally[:, :k * LOW] = tally[:, :k * LOW] + total
 
     def spread(store):
@@ -548,6 +569,15 @@
     mass_all[z] = jnp.zeros(mass_all.shape[1:], F32)
     counts = (c == 0) & (z < final)
 
+    def row_sums(error):
+        return lax.dot_general(
+            jnp.ones((8, span), F32), error * error, (((1,), (1,)), ((), ())),
+            precision=lax.Precision.HIGHEST, preferred_element_type=F32,
+        )
+
+    def up_copy(row, col):
+        return remote(loss_up.at[row], loss_in.at[z], up_send.at[row, col], up_recv.at[z], row, col)
+
     def part_copy(row):
         return remote(mass_sent, mass_own.at[slot], part_send.at[row], part_recv.at[slot], row, owner)
 
@@ -579,6 +609,13 @@
                     return take(source, shift + low - tile + lane[:chunk] // 2)
 
                 count(err_block.at[q], code_at)
+
+            @pl.when((g > z) & (q % PIECES == PIECES - 1))
+            def _():
+                error = jnp.concatenate([err_block[q - PIECES + 1 + h] for h in range(PIECES)], axis=0)
+                loss_up[g, :, :rows] = row_sums(error)
+                for col in range(nc):
+                    up_copy(g, col).start()
 
             return 0
 
@@ -616,6 +653,11 @@
                 )
             own_spread(j)
 
+        if j == 0:
+            @pl.when(is_last & (z == 0))
+            def _():
+                send_up()
+
     @pl.when(is_last & (z > 0))
     def _():
         j = m - 1
@@ -638,7 +680,17 @@
         def _():
             mass_copy(row).start()
 
-    loss = jnp.zeros((8, rows), F32)
+    loss_all[c] = jnp.zeros(loss_all.shape[1:], F32)
+    for j in range(m):
+        @pl.when((c * m + j >= z) & ((c * m + j < final) | is_last))
+        def _():
+            loss_all[c, :, :rows] = loss_all[c, :, :rows] + row_sums(err_own[j])
+
+    for col in range(nc):
+        @pl.when(col != c)
+        def _():
+            loss_copy(col).start()
+
     for j in reversed(range(m)):
         @pl.when(c * m + j < z)
         def _():
@@ -646,19 +698,7 @@
                 for h in range(PIECES):
                     arrived(err_own.at[j, h * piece:(h + 1) * piece], own_recv.at[j, h])
 
-        error = err_own[j]
-        errors_out[:, j * span:(j + 1) * span] = error
-        squared = error * error
-        loss = loss + lax.dot_general(
-            jnp.ones((8, span), F32), squared, (((1,), (1,)), ((), ())),
-            precision=lax.Precision.HIGHEST, preferred_element_type=F32,
-        )
-    loss_all[c, :, :rows] = loss
-
-    for col in range(nc):
-        @pl.when(col != c)
-        def _():
-            loss_copy(col).start()
+        errors_out[:, j * span:(j + 1) * span] = err_own[j]
 
     for j in range(m):
         @pl.when(c * m + j < z)
@@ -696,9 +736,9 @@
             def _():
                 core_copy(q, col).wait_send()
 
-        down = is_owner & ((g < z) | ((g > z) & early_up))
-
-        @pl.when(down | (is_last & (z < final) & (g > z) & jnp.logical_not(early_up)))
+        early = early_up(g)
+
+        @pl.when((is_owner & ((g < z) | ((g > z) & early))) | (is_last & (z < final) & (g > z) & jnp.logical_not(early)))
         def _():
             own_copy(q).wait_send()
 
@@ -711,6 +751,24 @@
     def _():
         for h in range(PIECES):
             zero_copy(h).wait_send()
+
+    for row in range(nr):
+        @pl.when(row != z)
+        def _():
+            mass_copy(row).wait_send()
+
+        @pl.when(part_remote(row))
+        def _():
+            part_copy(row).wait_send()
+
+        @pl.when(counts & (row > z))
+        def _():
+            for col in range(nc):
+                up_copy(row, col).wait_send()
+    for col in range(nc):
+        @pl.when(col != c)
+        def _():
+            loss_copy(col).wait_send()
 
     for col in range(nc):
         @pl.when(col != c)
@@ -721,6 +779,12 @@
     for col in range(1, nc):
         loss_sum = loss_sum + loss_all[col, 0:1, :rows]
     loss_out[...] = loss_sum
+    for row in range(final):
+        @pl.when(row < z)
+        def _():
+            with scope("wait_loss_up"):
+                arrived(loss_in.at[row], up_recv.at[row])
+            loss_out[...] = loss_out[...] + loss_in[row, 0:1, :rows]
 
     for row in range(nr):
         @pl.when(row != z)
@@ -739,19 +803,6 @@
                 with scope("wait_mass_part"):
                     arrived(mass_own.at[j], part_recv.at[j])
             mass_out[j * k:(j + 1) * k, :] = mass_out[j * k:(j + 1) * k, :] + mass_own[j]
-
-    for row in range(nr):
-        @pl.when(row != z)
-        def _():
-            mass_copy(row).wait_send()
-
-        @pl.when(part_remote(row))
-        def _():
-            part_copy(row).wait_send()
-    for col in range(nc):
-        @pl.when(col != c)
-        def _():
-            loss_copy(col).wait_send()
 
 
 def store(errors, loss, mass, errors_out, loss_out, mass_out, sems):
@@ -814,6 +865,8 @@
             pltpu.VMEM((m, k, code_count), F32),
             pltpu.VMEM((k, code_count), F32),
             pltpu.VMEM((nc, 8, max(rows, 128)), F32),
+            pltpu.VMEM((nr, 8, max(rows, 128)), F32),
+            pltpu.VMEM((nr, 8, max(rows, 128)), F32),
             dma((5,)),
             dma((m, PIECES)), dma((nr, PIECES)),
             dma((m,)), dma((nr,)),
@@ -824,7 +877,8 @@
             dma((steps,)), dma((m, PIECES)), dma((PIECES,)),
             dma((nr,)), dma((m,)),
             dma((nr,)), dma((nr,)),
-            dma((nc,)), dma((nc,)), pltpu.SemaphoreType.REGULAR,
+            dma((nc,)), dma((nc,)),
+            dma((nr, nc)), dma((nr,)), pltpu.SemaphoreType.REGULAR,
         ],
         compiler_params=pltpu.CompilerParams(
             collective_id=0, has_side_effects=True, vmem_limit_bytes=40 * 1024 * 1024

time: 35.9 us -> 33.8 us (0.942)
  the two profiles are of different devices: /device:TPU:29 before, /device:TPU:30 now
where the time goes in v5:
time: 33.8 us; the launch traced here: 33.6 us
  Pallas kernels  33 us (98%)
  between operations  0.64 us (2%)
    pallas_call x1, Pallas kernels, local(): pl.pallas_call(functools.partial(kernel, nr, nc), out_shape=tuple((pltpu....  32.3 us
    pallas_call x1, Pallas kernels, local(): pl.pallas_call(store, out_shape=tuple((jax.ShapeDtypeStruct(shape, F32) f...  0.74 us

profile of v5, /device:TPU:30, one launch (start us, length us, event | category | flops | bytes accessed | tf_op | source)
XLA Modules:
  0.0 33.6 jit_solution(18160682155601046480)
XLA Ops:
  0.6 32.3 %shard_map.76 = (f32[64,1024]{1,0:T(8,128)S(1)}, f32[1,64]{1,0:T(1,128)S(1)}, f32[8,256]{1,0:T(8,128)S(1)}) custom-call(f32[64,1024]{1,0:T(8,128)} %bitcast.9, f32[8,2,256]{2,1,0:T(2,128)} %bitcast.11, s32[64,512]{1,0:T(8,128)} %bitcast.10, f32[8,128,128]{2,1,0:T(8,128)} %bitcast.8, f32[512,1024]{1,0:T(8,128)} %bitcast.7), custom_call_target="tpu_custom_call" | custom-call | tf_op jit(solution)/shard_map/pallas_call | solution.py:832
  32.9 0.7 %shard_map.77 = (f32[64,1024]{1,0:T(8,128)}, f32[1,64]{1,0:T(1,128)}, f32[8,256]{1,0:T(8,128)}) custom-call(f32[64,1024]{1,0:T(8,128)S(1)} %get-tuple-element.9.errors, f32[1,64]{1,0:T(1,128)S(1)} %get-tuple-element.10.loss, f32[8,256]{1,0:T(8,128)S(1)} %get-tuple-element.11.mass), custom_call_target="tpu_custom_call" | custom-call | tf_op jit(solution)/shard_map/pallas_call | solution.py:889

commit v6 on v5

--- a/solution.py
+++ b/solution.py
@@ -81,8 +81,14 @@
         pltpu.make_async_copy(source, target, u_sem.at[number])
         for number, (source, target) in enumerate((
             (assign_hbm, assign), (codebook_hbm, codebook), (weights_hbm, weights),
-            (inverse_hbm, inverse), (factor, u_raw),
+            (inverse_hbm, inverse),
         ))
+    ]
+    loads += [
+        pltpu.make_async_copy(
+            factor.at[:, j * span:(j + 1) * span], u_raw.at[:, j * span:(j + 1) * span], u_sem.at[4 + j]
+        )
+        for j in range(m)
     ]
     for load in loads:
         load.start()
@@ -115,7 +121,7 @@
         return order(q // PIECES)
 
     def early_up(g):
-        return (z > 0) & (owner < nc - 1) & (g == nr)
+        return (z > 0) & (owner < nc - 1) & (g == nr - 1)
 
     def farthest(i):
         return order(nr - 1 - i // PIECES) * PIECES + i % PIECES
@@ -132,7 +138,7 @@
 
     def delta_copy(j, h):
         at = slice(h * piece, (h + 1) * piece)
-        return remote(delta.at[j, at], delta_in.at[z, at], d_send.at[j, h], d_recv.at[z, h], c * m + j, c)
+        return remote(delta.at[j, at], delta_in.at[z, at], d_send.at[j], d_recv.at[z, h], c * m + j, c)
 
     def send_delta(j, when):
         @pl.when((c * m + j < z) & when)
@@ -157,11 +163,11 @@
         return remote(
             u_raw.at[i * block:(i + 1) * block, low + (i + 1) * block:low + span],
             triangle.at[i * block:(i + 1) * block, (i + 1) * block:span],
-            tri_send.at[row, i], tri_recv.at[i], row, c,
+            tri_send, tri_recv, row, c,
         )
 
     def run_copy(q, j):
-        return remote(run_out.at[q, j], run_in.at[q, j], run_send.at[q, j], run_recv.at[q, j], z + 1, c)
+        return remote(run_out.at[q, j], run_in.at[q, j], run_send.at[j], run_recv.at[q, j], z + 1, c)
 
     def first(g):
         return jnp.where(g == 0, 1, 0)
@@ -170,20 +176,20 @@
         return jnp.maximum(g, 1)
 
     def last_copy(q):
-        at = first(group(q)), z, q % PIECES
-        return remote(last_out.at[q], last_in.at[at], last_send.at[q], last_recv.at[at], solver(group(q)), c)
+        which, h = first(group(q)), q % PIECES
+        return remote(last_out.at[q], last_in.at[which, h, z], last_send, last_recv.at[which, h], solver(group(q)), c)
 
     def zero_sum(q):
-        return remote(last_out.at[q], zero_in.at[q], last_send.at[q], zero_recv.at[q], 1, c)
+        return remote(last_out.at[q], zero_in.at[q], last_send, zero_recv.at[q], 1, c)
 
     def zero_copy(h):
         return remote(
             err_zero.at[h], err_own.at[m - 1, h * piece:(h + 1) * piece],
-            zero_send.at[h], own_recv.at[m - 1, h], 0, c,
+            zero_send, own_recv.at[m - 1, h], 0, c,
         )
 
     def core_copy(q, col):
-        return remote(err_block.at[q], err_block.at[q], core_send.at[q, col], core_recv.at[q], z, col)
+        return remote(err_block.at[q], err_block.at[q], core_send.at[col], core_recv.at[q], z, col)
 
     def own_copy(q):
         return remote(
@@ -231,19 +237,9 @@
                     ready, inc=1, device_id={"row": row, "col": col}, device_id_type=pl.DeviceIdType.MESH,
                 )
 
-    with scope("factor_loads"):
-        for load in loads[3:]:
-            load.wait()
-
     def rest():
         for j in range(1, m):
             subtract(j)
-
-    @pl.when((z == final) & is_last)
-    def _():
-        for row in reversed(range(1, final)):
-            for i in range(k - 1):
-                tri_copy(row, i).start()
 
     def inverted(first, right):
         v_full[...] = jnp.zeros_like(v_full)
@@ -264,6 +260,12 @@
 
     @pl.when(is_owner)
     def _():
+        with scope("factor_loads"):
+            loads[3].wait()
+            for j in range(m):
+                @pl.when(slot == j)
+                def _():
+                    loads[4 + j].wait()
         rest()
         base = slot * span
         high, low = inverted(slot * k, lambda top, middle, end: u_raw[
@@ -274,7 +276,22 @@
 
     @pl.when(jnp.logical_not(is_owner))
     def _():
+        loads[3].wait()
+        for j in range(m):
+            loads[4 + j].wait()
+
+        @pl.when((z == final) & is_last)
+        def _():
+            for row in reversed(range(1, final)):
+                for i in range(k - 1):
+                    tri_copy(row, i).start()
+
         rest()
+
+    for j in range(m):
+        @pl.when(is_owner & (slot != j))
+        def _():
+            loads[4 + j].wait()
 
     for j in range(m):
         @pl.when(c * m + j > z)
@@ -291,9 +308,8 @@
         @pl.when(z < final)
         def _():
             with scope("wait_triangle"):
-                for i in range(k - 1):
-                    part = triangle.at[i * block:(i + 1) * block, (i + 1) * block:span]
-                    arrived(part, tri_recv.at[i])
+                if k > 1:
+                    arrived(triangle.at[:block * (k - 1), :block * k // 2], tri_recv)
 
         high, low = inverted((m - 1) * k, lambda top, middle, end: triangle[top:middle, middle:end])
         w_high[...] = high
@@ -367,7 +383,7 @@
                 err_own[slot, at] = error
 
             for col in range(nc):
-                @pl.when((col > c) | ((col == 0) & (c > 0) & (g >= z)))
+                @pl.when((col > c) | ((col == 0) & (c > 0)))
                 def _():
                     core_copy(q, col).start()
 
@@ -395,7 +411,7 @@
 
             @pl.when((z > 1) & (solver(g) == z))
             def _():
-                last_in[first(g), z, q % PIECES] = change
+                last_in[first(g), q % PIECES, z] = change
 
             @pl.when((z > 1) & (solver(g) != z))
             def _():
@@ -473,19 +489,39 @@
 
         lax.fori_loop(0, steps - 2 * PIECES, relayed, 0)
 
+    def send_up():
+        def upward(i, _):
+            q = nearest(i)
+
+            @pl.when((group(q) > z) & jnp.logical_not(early_up(group(q))))
+            def _():
+                own_copy(q).start()
+
+            return 0
+
+        lax.fori_loop(0, steps, upward, 0)
+
     @pl.when(is_last & (z > 0) & (z < final - 1))
     def _():
         invert_last()
+
+    @pl.when(is_last & (z > 0) & (z < final))
+    def _():
+        send_up()
 
     def solved(which, h):
         with scope("wait_last"):
-            for row in range(1, final):
-                @pl.when(row != z)
+            if nr > 3:
+                @pl.when(z < final)
                 def _():
-                    arrived(last_in.at[which, row, h], last_recv.at[which, row, h])
-        total = -last_in[which, 1, h]
+                    arrived(last_in.at[which, h, :nr - 3], last_recv.at[which, h])
+
+            @pl.when(z == final)
+            def _():
+                arrived(last_in.at[which, h, :nr - 2], last_recv.at[which, h])
+        total = -last_in[which, h, 1]
         for row in range(2, final):
-            total = total - last_in[which, row, h]
+            total = total - last_in[which, h, row]
         if which == 0:
             total = total + delta[m - 1, h * piece:(h + 1) * piece]
         return dot3(total, w_high[...], w_low[...])
@@ -493,28 +529,9 @@
     @pl.when(is_last & (z == 1))
     def _():
         for h in range(PIECES):
-            last_in[1, 1, h] = joined(h)
+            last_in[1, h, 1] = joined(h)
             err_zero[h] = solved(1, h)
             zero_copy(h).start()
-        for h in range(PIECES):
-            last_in[0, 1, h] = joined(PIECES + h)
-
-    def send_up():
-        def upward(i, _):
-            q = nearest(i)
-
-            @pl.when((group(q) > z) & jnp.logical_not(early_up(group(q))))
-            def _():
-                own_copy(q).start()
-
-            return 0
-
-        lax.fori_loop(0, steps, upward, 0)
-
-    @pl.when(is_last & (z > 0) & (z < final))
-    def _():
-        send_up()
-
     high_count = code_count // LOW
     fold = 2 * high_count
     chunk = 16
@@ -576,10 +593,10 @@
         )
 
     def up_copy(row, col):
-        return remote(loss_up.at[row], loss_in.at[z], up_send.at[row, col], up_recv.at[z], row, col)
+        return remote(loss_up.at[row], loss_in.at[z], up_send.at[row], up_recv.at[z], row, col)
 
     def part_copy(row):
-        return remote(mass_sent, mass_own.at[slot], part_send.at[row], part_recv.at[slot], row, owner)
+        return remote(mass_sent, mass_own.at[slot], part_send, part_recv.at[slot], row, owner)
 
     def part_remote(row):
         return counts & ((row != z) | (owner != 0))
@@ -589,13 +606,14 @@
         def own_part(q, _):
             g = group(q)
 
+            @pl.when(owner != 0)
+            def _():
+                with scope("wait_part"):
+                    arrived(err_block.at[q], core_recv.at[q])
+
             @pl.when(g >= z)
             def _():
-                with scope("wait_part"):
-                    @pl.when(owner != 0)
-                    def _():
-                        arrived(err_block.at[q], core_recv.at[q])
-
+                with scope("wait_code"):
                     @pl.when(((g != z) | (owner != 0)) & (q % PIECES == 0))
                     def _():
                         arrived(codes_in.at[g], code_recv.at[g])
@@ -661,6 +679,12 @@
     @pl.when(is_last & (z > 0))
     def _():
         j = m - 1
+
+        @pl.when(z == 1)
+        def _():
+            for h in range(PIECES):
+                last_in[0, h, 1] = joined(PIECES + h)
+
         for h in range(PIECES):
             err_own[j, h * piece:(h + 1) * piece] = solved(0, h)
             count(
@@ -670,10 +694,10 @@
         own_spread(j)
 
     def mass_copy(row):
-        return remote(mass_all.at[z], mass_all.at[z], mass_send.at[row], mass_recv.at[z], row, c)
+        return remote(mass_all.at[z], mass_all.at[z], mass_send, mass_recv, row, c)
 
     def loss_copy(col):
-        return remote(loss_all.at[c], loss_all.at[c], loss_send.at[col], loss_recv.at[c], z, col)
+        return remote(loss_all.at[c], loss_all.at[c], loss_send, loss_recv, z, col)
 
     for row in range(nr):
         @pl.when(row != z)
@@ -691,6 +715,77 @@
         def _():
             loss_copy(col).start()
 
+    for j in range(m):
+        @pl.when(c * m + j < z)
+        def _():
+            arrived(delta.at[j], d_send.at[j])
+
+        @pl.when(code_sent(j))
+        def _():
+            code_copy(j).wait_send()
+
+        @pl.when((c * m + j > z) & (c * m + j < final))
+        def _():
+            arrived(run_out.at[:, j], run_send.at[j])
+
+    if k > 1:
+        @pl.when((z == final) & is_last)
+        def _():
+            arrived(u_raw.at[:, :(nr - 2) * block * (k - 1) // 2], tri_send)
+
+    @pl.when(is_last & (z == 0))
+    def _():
+        arrived(last_out, last_send)
+
+    @pl.when(is_last & (z == 1))
+    def _():
+        arrived(last_out.at[:steps - 2 * PIECES], last_send)
+        arrived(err_zero, zero_send)
+
+    @pl.when(is_last & (z > 1) & (z < final))
+    def _():
+        arrived(last_out.at[:steps - PIECES], last_send)
+
+    for col in range(nc):
+        @pl.when(is_owner & ((col > c) | ((col == 0) & (c > 0))))
+        def _():
+            arrived(err_block, core_send.at[col])
+
+    @pl.when((is_owner | is_last) & (z < final))
+    def _():
+        def drain(q, _):
+            g = group(q)
+            early = early_up(g)
+
+            @pl.when((is_owner & ((g < z) | ((g > z) & early))) | (is_last & (g > z) & jnp.logical_not(early)))
+            def _():
+                own_copy(q).wait_send()
+
+            return 0
+
+        with scope("drain"):
+            lax.fori_loop(0, steps, drain, 0)
+
+    part_size = mass_all.at[:, :k]
+
+    @pl.when(counts)
+    def _():
+        for row in range(nr):
+            @pl.when(row > z)
+            def _():
+                arrived(loss_all, up_send.at[row])
+
+        @pl.when(owner == 0)
+        def _():
+            arrived(part_size.at[:nr - 1], part_send)
+
+        @pl.when(owner != 0)
+        def _():
+            arrived(part_size, part_send)
+
+    arrived(mass_all.at[:nr - 1], mass_send)
+    arrived(loss_all.at[:nc - 1], loss_send)
+
     for j in reversed(range(m)):
         @pl.when(c * m + j < z)
         def _():
@@ -700,81 +795,8 @@
 
         errors_out[:, j * span:(j + 1) * span] = err_own[j]
 
-    for j in range(m):
-        @pl.when(c * m + j < z)
-        def _():
-            for h in range(PIECES):
-                delta_copy(j, h).wait_send()
-
-        @pl.when(code_sent(j))
-        def _():
-            code_copy(j).wait_send()
-
-    @pl.when((z == final) & is_last)
-    def _():
-        for row in range(1, final):
-            for i in range(k - 1):
-                tri_copy(row, i).wait_send()
-
-    def drain(q, _):
-        g = group(q)
-        for j in range(m):
-            @pl.when((c * m + j > z) & (c * m + j < final))
-            def _():
-                run_copy(q, j).wait_send()
-
-        @pl.when(is_last & (z == 0))
-        def _():
-            zero_sum(q).wait_send()
-
-        @pl.when(is_last & (z > 0) & (z < final) & (solver(g) != z))
-        def _():
-            last_copy(q).wait_send()
-
-        for col in range(nc):
-            @pl.when(is_owner & ((col > c) | ((col == 0) & (c > 0) & (g >= z))))
-            def _():
-                core_copy(q, col).wait_send()
-
-        early = early_up(g)
-
-        @pl.when((is_owner & ((g < z) | ((g > z) & early))) | (is_last & (z < final) & (g > z) & jnp.logical_not(early)))
-        def _():
-            own_copy(q).wait_send()
-
-        return 0
-
-    with scope("drain"):
-        lax.fori_loop(0, steps, drain, 0)
-
-    @pl.when(is_last & (z == 1))
-    def _():
-        for h in range(PIECES):
-            zero_copy(h).wait_send()
-
-    for row in range(nr):
-        @pl.when(row != z)
-        def _():
-            mass_copy(row).wait_send()
-
-        @pl.when(part_remote(row))
-        def _():
-            part_copy(row).wait_send()
-
-        @pl.when(counts & (row > z))
-        def _():
-            for col in range(nc):
-                up_copy(row, col).wait_send()
-    for col in range(nc):
-        @pl.when(col != c)
-        def _():
-            loss_copy(col).wait_send()
-
-    for col in range(nc):
-        @pl.when(col != c)
-        def _():
-            with scope("wait_loss"):
-                arrived(loss_all.at[col], loss_recv.at[col])
+    with scope("wait_loss"):
+        arrived(loss_all.at[:nc - 1], loss_recv)
     loss_sum = loss_all[0, 0:1, :rows]
     for col in range(1, nc):
         loss_sum = loss_sum + loss_all[col, 0:1, :rows]
@@ -786,11 +808,14 @@
                 arrived(loss_in.at[row], up_recv.at[row])
             loss_out[...] = loss_out[...] + loss_in[row, 0:1, :rows]
 
-    for row in range(nr):
-        @pl.when(row != z)
-        def _():
-            with scope("wait_mass"):
-                arrived(mass_all.at[row], mass_recv.at[row])
+    for j in range(m):
+        @pl.when((c * m + j < final) & ((c * m + j != z) | (c != 0)))
+        def _():
+            with scope("wait_mass_part"):
+                arrived(mass_own.at[j], part_recv.at[j])
+
+    with scope("wait_mass"):
+        arrived(mass_all.at[:nr - 1], mass_recv)
     mass_sum = mass_all[0]
     for row in range(1, nr):
         mass_sum = mass_sum + mass_all[row]
@@ -798,10 +823,6 @@
     for j in range(m):
         @pl.when(c * m + j < final)
         def _():
-            @pl.when((c * m + j != z) | (c != 0))
-            def _():
-                with scope("wait_mass_part"):
-                    arrived(mass_own.at[j], part_recv.at[j])
             mass_out[j * k:(j + 1) * k, :] = mass_out[j * k:(j + 1) * k, :] + mass_own[j]
 
 
@@ -824,7 +845,6 @@
     blocks, code_count = codebook.shape[1], codebook.shape[3]
     block = inv_blocks.shape[2]
     k = span // block
-    edges = max(k - 1, 1)
     dma = pltpu.SemaphoreType.DMA
     vmem = pl.BlockSpec(memory_space=pltpu.VMEM)
     hbm = pl.BlockSpec(memory_space=pltpu.HBM)
@@ -854,7 +874,7 @@
             pltpu.VMEM((nr, rows, max(span // 2, block)), jnp.int32),
             pltpu.VMEM((steps, m, piece, span), F32),
             pltpu.VMEM((steps, m, piece, span), F32),
-            pltpu.VMEM((2, nr, PIECES, piece, span), F32),
+            pltpu.VMEM((2, PIECES, nr, piece, span), F32),
             pltpu.VMEM((steps, piece, span), F32),
             pltpu.VMEM((steps, piece, span), F32),
             pltpu.VMEM((steps, piece, span), F32),
@@ -867,18 +887,18 @@
             pltpu.VMEM((nc, 8, max(rows, 128)), F32),
             pltpu.VMEM((nr, 8, max(rows, 128)), F32),
             pltpu.VMEM((nr, 8, max(rows, 128)), F32),
-            dma((5,)),
-            dma((m, PIECES)), dma((nr, PIECES)),
+            dma((4 + m,)),
+            dma((m,)), dma((nr, PIECES)),
             dma((m,)), dma((nr,)),
-            dma((nr, edges)), dma((edges,)),
-            dma((steps, m)), dma((steps, m)),
-            dma((steps,)), dma((2, nr, PIECES)), dma((steps,)),
-            dma((steps, nc)), dma((steps,)),
-            dma((steps,)), dma((m, PIECES)), dma((PIECES,)),
-            dma((nr,)), dma((m,)),
-            dma((nr,)), dma((nr,)),
-            dma((nc,)), dma((nc,)),
-            dma((nr, nc)), dma((nr,)), pltpu.SemaphoreType.REGULAR,
+            dma, dma,
+            dma((m,)), dma((steps, m)),
+            dma, dma((2, PIECES)), dma((steps,)),
+            dma((nc,)), dma((steps,)),
+            dma((steps,)), dma((m, PIECES)), dma,
+            dma, dma((m,)),
+            dma, dma,
+            dma, dma,
+            dma((nr,)), dma((nr,)), pltpu.SemaphoreType.REGULAR,
         ],
         compiler_params=pltpu.CompilerParams(
             collective_id=0, has_side_effects=True, vmem_limit_bytes=40 * 1024 * 1024

time: 33.8 us -> 31.4 us (0.929)
  the two profiles are of different devices: /device:TPU:30 before, /device:TPU:1 now
where the time goes in v6:
time: 31.4 us; the launch traced here: 31.3 us
  Pallas kernels  30.7 us (98%)
  between operations  0.64 us (2%)
    pallas_call x1, Pallas kernels, local(): pl.pallas_call(functools.partial(kernel, nr, nc), out_shape=tuple((pltpu....  29.9 us
    pallas_call x1, Pallas kernels, local(): pl.pallas_call(store, out_shape=tuple((jax.ShapeDtypeStruct(shape, F32) f...  0.74 us

profile of v6, /device:TPU:1, one launch (start us, length us, event | category | flops | bytes accessed | tf_op | source)
XLA Modules:
  0.0 31.3 jit_solution(5271449193583743200)
XLA Ops:
  0.6 29.9 %shard_map.76 = (f32[64,1024]{1,0:T(8,128)S(1)}, f32[1,64]{1,0:T(1,128)S(1)}, f32[8,256]{1,0:T(8,128)S(1)}) custom-call(f32[64,1024]{1,0:T(8,128)} %bitcast.9, f32[8,2,256]{2,1,0:T(2,128)} %bitcast.11, s32[64,512]{1,0:T(8,128)} %bitcast.10, f32[8,128,128]{2,1,0:T(8,128)} %bitcast.8, f32[512,1024]{1,0:T(8,128)} %bitcast.7), custom_call_target="tpu_custom_call" | custom-call | tf_op jit(solution)/shard_map/pallas_call | solution.py:852
  30.6 0.7 %shard_map.77 = (f32[64,1024]{1,0:T(8,128)}, f32[1,64]{1,0:T(1,128)}, f32[8,256]{1,0:T(8,128)}) custom-call(f32[64,1024]{1,0:T(8,128)S(1)} %get-tuple-element.9.errors, f32[1,64]{1,0:T(1,128)S(1)} %get-tuple-element.10.loss, f32[8,256]{1,0:T(8,128)S(1)} %get-tuple-element.11.mass), custom_call_target="tpu_custom_call" | custom-call | tf_op jit(solution)/shard_map/pallas_call | solution.py:909

commit v7 on v6

--- a/solution.py
+++ b/solution.py
@@ -44,9 +44,9 @@
     weights_hbm, codebook_hbm, assign_hbm, inverse_hbm, factor,
     errors_out, loss_out, mass_out,
     weights, codebook, assign, inverse, u_raw, u_high, u_low, triangle, v_full, v_high, v_low, w_high, w_low,
-    delta, codes, delta_in, codes_in, run_in, run_out, last_in, last_out, zero_in,
+    delta, codes, delta_in, codes_in, run_in, run_out, last_in, last_out,
     err_block, err_own, err_zero, tally, mass_all, mass_own, mass_sent, loss_all, loss_up, loss_in,
-    u_sem, d_send, d_recv, code_send, code_recv, tri_send, tri_recv, run_send, run_recv, last_send, last_recv, zero_recv,
+    u_sem, d_send, code_send, code_recv, tri_send, tri_recv, run_send, run_recv, last_send, last_recv,
     core_send, core_recv, own_send, own_recv, zero_send, part_send, part_recv, mass_send, mass_recv,
     loss_send, loss_recv, up_send, up_recv, ready,
 ):
@@ -138,7 +138,7 @@
 
     def delta_copy(j, h):
         at = slice(h * piece, (h + 1) * piece)
-        return remote(delta.at[j, at], delta_in.at[z, at], d_send.at[j], d_recv.at[z, h], c * m + j, c)
+        return remote(delta.at[j, at], delta_in.at[z, at], d_send.at[j], core_recv.at[z * PIECES + h], c * m + j, c)
 
     def send_delta(j, when):
         @pl.when((c * m + j < z) & when)
@@ -152,7 +152,7 @@
     def code_copy(j):
         low = j * pairs // window * window
         return remote(
-            assign.at[:, low:low + window], codes_in.at[z], code_send.at[j], code_recv.at[z], c * m + j, 0
+            assign.at[:, low:low + window], codes_in.at[z], code_send.at[j], code_recv, c * m + j, 0
         )
 
     def code_sent(j):
@@ -180,7 +180,7 @@
         return remote(last_out.at[q], last_in.at[which, h, z], last_send, last_recv.at[which, h], solver(group(q)), c)
 
     def zero_sum(q):
-        return remote(last_out.at[q], zero_in.at[q], last_send, zero_recv.at[q], 1, c)
+        return remote(last_out.at[q], run_in.at[q, m - 1], last_send, run_recv.at[q, m - 1], 1, c)
 
     def zero_copy(h):
         return remote(
@@ -194,7 +194,7 @@
     def own_copy(q):
         return remote(
             err_block.at[q], err_own.at[slot, part_rows(q)],
-            own_send.at[q], own_recv.at[slot, q % PIECES], group(q), owner,
+            own_send, own_recv.at[slot, q % PIECES], group(q), owner,
         )
 
     with scope("first_loads"):
@@ -345,7 +345,9 @@
         g = group(q)
         at = part_rows(q)
 
-        @pl.when(is_last & (((z == final) & (q == 0)) | ((z == final - 1) & (q == PIECES))))
+        turn = jnp.where(z == final, 0, PIECES)
+
+        @pl.when(is_last & (z >= final - 1) & (q == turn))
         def _():
             invert_last()
 
@@ -367,7 +369,7 @@
             @pl.when(g > z)
             def _():
                 with scope("wait_delta"):
-                    arrived(delta_in.at[g, at], d_recv.at[g, q % PIECES])
+                    arrived(delta_in.at[g, at], core_recv.at[g * PIECES + q % PIECES])
 
                 run_in[q, slot] = run_in[q, slot] + delta_in[g, at]
 
@@ -476,8 +478,12 @@
 
     def joined(q):
         with scope("wait_zero"):
-            arrived(zero_in.at[q], zero_recv.at[q])
-        return last_out[q] + zero_in[q]
+            arrived(run_in.at[q, m - 1], run_recv.at[q, m - 1])
+        return last_out[q] + run_in[q, m - 1]
+
+    @pl.when(is_last & (z > 0) & (z < final - 1))
+    def _():
+        invert_last()
 
     @pl.when(is_last & (z == 1) & (z < final))
     def _():
@@ -501,11 +507,12 @@
 
         lax.fori_loop(0, steps, upward, 0)
 
-    @pl.when(is_last & (z > 0) & (z < final - 1))
-    def _():
-        invert_last()
-
-    @pl.when(is_last & (z > 0) & (z < final))
+    @pl.when(is_last & (z == 0))
+    def _():
+        with scope("wait_left"):
+            arrived(last_out, last_send)
+
+    @pl.when(is_last & (z < final))
     def _():
         send_up()
 
@@ -593,7 +600,7 @@
         )
 
     def up_copy(row, col):
-        return remote(loss_up.at[row], loss_in.at[z], up_send.at[row], up_recv.at[z], row, col)
+        return remote(loss_up.at[row], loss_in.at[z], up_send, up_recv, row, col)
 
     def part_copy(row):
         return remote(mass_sent, mass_own.at[slot], part_send, part_recv.at[slot], row, owner)
@@ -601,6 +608,15 @@
     def part_remote(row):
         return counts & ((row != z) | (owner != 0))
 
+    for row in range(final):
+        for other in range(2):
+            number = final - row + other
+
+            @pl.when(counts & (z == row) & ((owner != 0) == (other == 1)))
+            def _():
+                with scope("wait_code"):
+                    arrived(codes_in.at[:number], code_recv)
+
     @pl.when(counts)
     def _():
         def own_part(q, _):
@@ -613,11 +629,6 @@
 
             @pl.when(g >= z)
             def _():
-                with scope("wait_code"):
-                    @pl.when(((g != z) | (owner != 0)) & (q % PIECES == 0))
-                    def _():
-                        arrived(codes_in.at[g], code_recv.at[g])
-
                 shift = 0 if window == pairs else lax.rem(slot * pairs, window)
 
                 def code_at(b, at):
@@ -671,11 +682,6 @@
                 )
             own_spread(j)
 
-        if j == 0:
-            @pl.when(is_last & (z == 0))
-            def _():
-                send_up()
-
     @pl.when(is_last & (z > 0))
     def _():
         j = m - 1
@@ -699,10 +705,11 @@
     def loss_copy(col):
         return remote(loss_all.at[c], loss_all.at[c], loss_send, loss_recv, z, col)
 
-    for row in range(nr):
-        @pl.when(row != z)
-        def _():
-            mass_copy(row).start()
+    with scope("send_mass"):
+        for row in range(nr):
+            @pl.when(row != z)
+            def _():
+                mass_copy(row).start()
 
     loss_all[c] = jnp.zeros(loss_all.shape[1:], F32)
     for j in range(m):
@@ -733,10 +740,6 @@
         def _():
             arrived(u_raw.at[:, :(nr - 2) * block * (k - 1) // 2], tri_send)
 
-    @pl.when(is_last & (z == 0))
-    def _():
-        arrived(last_out, last_send)
-
     @pl.when(is_last & (z == 1))
     def _():
         arrived(last_out.at[:steps - 2 * PIECES], last_send)
@@ -751,29 +754,30 @@
         def _():
             arrived(err_block, core_send.at[col])
 
-    @pl.when((is_owner | is_last) & (z < final))
-    def _():
-        def drain(q, _):
-            g = group(q)
-            early = early_up(g)
-
-            @pl.when((is_owner & ((g < z) | ((g > z) & early))) | (is_last & (g > z) & jnp.logical_not(early)))
-            def _():
-                own_copy(q).wait_send()
-
-            return 0
-
-        with scope("drain"):
-            lax.fori_loop(0, steps, drain, 0)
+    for row in range(final):
+        early = 1 if row > 0 and row // m < nc - 1 else 0
+        up = final - row - early
+        both = row // m == nc - 1
+
+        @pl.when((z == row) & is_owner)
+        def _():
+            number = row + early + (up if both else 0)
+            if number:
+                arrived(err_block.at[:number * PIECES], own_send)
+
+        if not both and up:
+            @pl.when((z == row) & is_last)
+            def _():
+                arrived(err_block.at[:up * PIECES], own_send)
 
     part_size = mass_all.at[:, :k]
 
     @pl.when(counts)
     def _():
-        for row in range(nr):
-            @pl.when(row > z)
-            def _():
-                arrived(loss_all, up_send.at[row])
+        for row in range(final):
+            @pl.when(z == row)
+            def _():
+                arrived(loss_up.at[:(final - row) * nc], up_send)
 
         @pl.when(owner == 0)
         def _():
@@ -801,12 +805,15 @@
     for col in range(1, nc):
         loss_sum = loss_sum + loss_all[col, 0:1, :rows]
     loss_out[...] = loss_sum
-    for row in range(final):
-        @pl.when(row < z)
+    for row in range(1, nr):
+        @pl.when(z == row)
         def _():
             with scope("wait_loss_up"):
-                arrived(loss_in.at[row], up_recv.at[row])
-            loss_out[...] = loss_out[...] + loss_in[row, 0:1, :rows]
+                arrived(loss_in.at[:row], up_recv)
+            total = loss_out[...]
+            for lower in range(row):
+                total = total + loss_in[lower, 0:1, :rows]
+            loss_out[...] = total
 
     for j in range(m):
         @pl.when((c * m + j < final) & ((c * m + j != z) | (c != 0)))
@@ -877,7 +884,6 @@
             pltpu.VMEM((2, PIECES, nr, piece, span), F32),
             pltpu.VMEM((steps, piece, span), F32),
             pltpu.VMEM((steps, piece, span), F32),
-            pltpu.VMEM((steps, piece, span), F32),
             pltpu.VMEM((m, rows, span), F32),
             pltpu.VMEM((PIECES, piece, span), F32),
             pltpu.VMEM((k * 2 * (code_count // LOW), block), F32),
@@ -885,20 +891,20 @@
             pltpu.VMEM((m, k, code_count), F32),
             pltpu.VMEM((k, code_count), F32),
             pltpu.VMEM((nc, 8, max(rows, 128)), F32),
-            pltpu.VMEM((nr, 8, max(rows, 128)), F32),
+            pltpu.VMEM((nr * nc, 8, max(rows, 128)), F32),
             pltpu.VMEM((nr, 8, max(rows, 128)), F32),
             dma((4 + m,)),
-            dma((m,)), dma((nr, PIECES)),
-            dma((m,)), dma((nr,)),
+            dma((m,)),
+            dma((m,)), dma,
             dma, dma,
             dma((m,)), dma((steps, m)),
-            dma, dma((2, PIECES)), dma((steps,)),
+            dma, dma((2, PIECES)),
             dma((nc,)), dma((steps,)),
-            dma((steps,)), dma((m, PIECES)), dma,
+            dma, dma((m, PIECES)), dma,
             dma, dma((m,)),
             dma, dma,
             dma, dma,
-            dma((nr,)), dma((nr,)), pltpu.SemaphoreType.REGULAR,
+            dma, dma, pltpu.SemaphoreType.REGULAR,
         ],
         compiler_params=pltpu.CompilerParams(
             collective_id=0, has_side_effects=True, vmem_limit_bytes=40 * 1024 * 1024

time: 31.4 us -> 30.9 us (0.984)
  Pallas kernels: 30.7 us -> 30.1 us
    pallas_call x1, Pallas kernels: 29.9 us -> 29.4 us  [local(): pl.pallas_call(functools.partial(kernel, nr, nc), out_shape=tuple((pltpu....]
where the time goes in v7:
time: 30.9 us; the launch traced here: 30.8 us
  Pallas kernels  30.1 us (97%)
  between operations  0.64 us (2%)
    pallas_call x1, Pallas kernels, local(): pl.pallas_call(functools.partial(kernel, nr, nc), out_shape=tuple((pltpu....  29.4 us
    pallas_call x1, Pallas kernels, local(): pl.pallas_call(store, out_shape=tuple((jax.ShapeDtypeStruct(shape, F32) f...  0.74 us

profile of v7, /device:TPU:1, one launch (start us, length us, event | category | flops | bytes accessed | tf_op | source)
XLA Modules:
  0.0 30.8 jit_solution(11237651589603860993)
XLA Ops:
  0.6 29.4 %shard_map.76 = (f32[64,1024]{1,0:T(8,128)S(1)}, f32[1,64]{1,0:T(1,128)S(1)}, f32[8,256]{1,0:T(8,128)S(1)}) custom-call(f32[64,1024]{1,0:T(8,128)} %bitcast.9, f32[8,2,256]{2,1,0:T(2,128)} %bitcast.11, s32[64,512]{1,0:T(8,128)} %bitcast.10, f32[8,128,128]{2,1,0:T(8,128)} %bitcast.8, f32[512,1024]{1,0:T(8,128)} %bitcast.7), custom_call_target="tpu_custom_call" | custom-call | tf_op jit(solution)/shard_map/pallas_call | solution.py:859
  30.0 0.7 %shard_map.77 = (f32[64,1024]{1,0:T(8,128)}, f32[1,64]{1,0:T(1,128)}, f32[8,256]{1,0:T(8,128)}) custom-call(f32[64,1024]{1,0:T(8,128)S(1)} %get-tuple-element.9.errors, f32[1,64]{1,0:T(1,128)S(1)} %get-tuple-element.10.loss, f32[8,256]{1,0:T(8,128)S(1)} %get-tuple-element.11.mass), custom_call_target="tpu_custom_call" | custom-call | tf_op jit(solution)/shard_map/pallas_call | solution.py:915

commit v8 on v7

--- a/solution.py
+++ b/solution.py
@@ -95,7 +95,7 @@
 
     barrier = pltpu.get_barrier_semaphore()
     for step in range(1, nr * nc):
-        other = lax.rem(z * nc + c + step, nr * nc)
+        other = lax.rem(z * nc + c + nr * nc - step, nr * nc)
 
         @pl.when(z <= other // nc + 1)
         def _():
@@ -451,49 +451,62 @@
     def _():
         wait_ready()
 
-    for j in range(m):
-        @pl.when(late_core & (c * m + j < final))
-        def _():
-            def release(q, _):
-                run_copy(q, j).start()
-                return 0
-
-            lax.fori_loop(2 * PIECES, steps, release, 0)
-
-        @pl.when(relay_core & (c * m + j < final))
-        def _():
-            def release(q, _):
-                forward(q, j)
-                return 0
-
-            lax.fori_loop(steps - PIECES, steps, release, 0)
-
-    @pl.when(late_core & is_last)
-    def _():
-        def release(i, _):
-            zero_sum(zero_order(i)).start()
-            return 0
-
-        lax.fori_loop(0, steps, release, 0)
-
     def joined(q):
         with scope("wait_zero"):
             arrived(run_in.at[q, m - 1], run_recv.at[q, m - 1])
         return last_out[q] + run_in[q, m - 1]
 
+    def contribute(low, high):
+        @pl.when(late_core & is_last)
+        def _():
+            def release(i, _):
+                zero_sum(zero_order(i)).start()
+                return 0
+
+            lax.fori_loop(low, high, release, 0)
+
+        @pl.when(is_last & (z == 1) & (z < final))
+        def _():
+            def relayed(i, _):
+                q = farthest(i)
+                last_out[q] = joined(q)
+                last_copy(q).start()
+                return 0
+
+            lax.fori_loop(low, min(high, steps - 2 * PIECES), relayed, 0)
+
+    for j in range(m):
+        @pl.when(late_core & (c * m + j < final))
+        def _():
+            def release(q, _):
+                run_copy(q, j).start()
+                return 0
+
+            lax.fori_loop(2 * PIECES, steps - PIECES, release, 0)
+
+    contribute(0, PIECES)
+
+    for j in range(m):
+        @pl.when((late_core | relay_core) & (c * m + j < final))
+        def _():
+            def release(q, _):
+                @pl.when(z > 0)
+                def _():
+                    forward(q, j)
+
+                @pl.when(z == 0)
+                def _():
+                    run_copy(q, j).start()
+
+                return 0
+
+            lax.fori_loop(steps - PIECES, steps, release, 0)
+
+    contribute(PIECES, steps)
+
     @pl.when(is_last & (z > 0) & (z < final - 1))
     def _():
         invert_last()
-
-    @pl.when(is_last & (z == 1) & (z < final))
-    def _():
-        def relayed(i, _):
-            q = farthest(i)
-            last_out[q] = joined(q)
-            last_copy(q).start()
-            return 0
-
-        lax.fori_loop(0, steps - 2 * PIECES, relayed, 0)
 
     def send_up():
         def upward(i, _):

time: 30.9 us -> 31.1 us (level); the launches traced: 30.8 us -> 30.6 us
  no operation moved by 1% of the time
where the time goes in v8:
time: 31.1 us; the launch traced here: 30.6 us
  Pallas kernels  30 us (96%)
  between operations  0.64 us (2%)
    pallas_call x1, Pallas kernels, local(): pl.pallas_call(functools.partial(kernel, nr, nc), out_shape=tuple((pltpu....  29.2 us
    pallas_call x1, Pallas kernels, local(): pl.pallas_call(store, out_shape=tuple((jax.ShapeDtypeStruct(shape, F32) f...  0.74 us

profile of v8, /device:TPU:1, one launch (start us, length us, event | category | flops | bytes accessed | tf_op | source)
XLA Modules:
  0.0 30.6 jit_solution(9623098735178876647)
XLA Ops:
  0.6 29.2 %shard_map.76 = (f32[64,1024]{1,0:T(8,128)S(1)}, f32[1,64]{1,0:T(1,128)S(1)}, f32[8,256]{1,0:T(8,128)S(1)}) custom-call(f32[64,1024]{1,0:T(8,128)} %bitcast.9, f32[8,2,256]{2,1,0:T(2,128)} %bitcast.11, s32[64,512]{1,0:T(8,128)} %bitcast.10, f32[8,128,128]{2,1,0:T(8,128)} %bitcast.8, f32[512,1024]{1,0:T(8,128)} %bitcast.7), custom_call_target="tpu_custom_call" | custom-call | tf_op jit(solution)/shard_map/pallas_call | solution.py:872
  29.9 0.7 %shard_map.77 = (f32[64,1024]{1,0:T(8,128)}, f32[1,64]{1,0:T(1,128)}, f32[8,256]{1,0:T(8,128)}) custom-call(f32[64,1024]{1,0:T(8,128)S(1)} %get-tuple-element.9.errors, f32[1,64]{1,0:T(1,128)S(1)} %get-tuple-element.10.loss, f32[8,256]{1,0:T(8,128)S(1)} %get-tuple-element.11.mass), custom_call_target="tpu_custom_call" | custom-call | tf_op jit(solution)/shard_map/pallas_call | solution.py:928
